TPU v7x, 16 devices: a whole 2x2x2 slice. The times are simulated.
16 devices in a mesh: rep: 1, dp: 16 (over x, y, z, core).
Axes of the slice: x: 2, y: 2, z: 2, core: 2. Of those that a mesh axis runs over, the one named last changes fastest.
Arguments:
- x: bfloat16 [16, 2048, 1280], P(('rep', 'dp'))
- dy: bfloat16 [16, 2048, 1280], P(('rep', 'dp'))
- w_gate: bfloat16 [2, 1280, 3072], replicated
- w_up: bfloat16 [2, 1280, 3072], replicated
- w_down: bfloat16 [2, 3072, 1280], replicated
- m_w_gate: float32 [2, 1280, 3072], P(None, 'dp')
- m_w_up: float32 [2, 1280, 3072], P(None, 'dp')
- m_w_down: float32 [2, 3072, 1280], P(None, 'dp')
- v_w_gate: float32 [2, 1280, 3072], P(None, 'dp')
- v_w_up: float32 [2, 1280, 3072], P(None, 'dp')
- v_w_down: float32 [2, 3072, 1280], P(None, 'dp')
Outputs:
- output 1: bfloat16 [2, 1280, 3072], P('rep')
- output 2: bfloat16 [2, 1280, 3072], P('rep')
- output 3: bfloat16 [2, 3072, 1280], P('rep')
- output 4: float32 [2, 1280, 3072], P('rep', 'dp')
- output 5: float32 [2, 1280, 3072], P('rep', 'dp')
- output 6: float32 [2, 3072, 1280], P('rep', 'dp')
- output 7: float32 [2, 1280, 3072], P('rep', 'dp')
- output 8: float32 [2, 1280, 3072], P('rep', 'dp')
- output 9: float32 [2, 3072, 1280], P('rep', 'dp')
All inputs are finite; a program needn't handle non-finite values.
Results may differ from a plain program's by a relative error of at most 0.022.
Values are sent between devices in bfloat16 or wider.
A program may use at most 2 GiB of HBM per device.

v0:
```python
import jax
import jax.numpy as jnp
from jax import lax

NAMES = ("w_gate", "w_up", "w_down")


def matmul(a, w):
    return jnp.dot(a, w, preferred_element_type=jnp.float32).astype(jnp.bfloat16)


def normed(h):
    wide = h.astype(jnp.float32)
    scale = lax.rsqrt(jnp.mean(wide**2, -1, keepdims=True) + 1e-6)
    return (wide * scale).astype(jnp.bfloat16)


def layer(h, w):
    a = normed(h)
    gate = jnp.dot(a, w["w_gate"], preferred_element_type=jnp.float32)
    up = jnp.dot(a, w["w_up"], preferred_element_type=jnp.float32)
    return h + matmul((jax.nn.silu(gate) * up).astype(jnp.bfloat16), w["w_down"])


def adamw(w, m, v, g):
    m = 0.9 * m + 0.1 * g
    v = 0.95 * v + 0.05 * g * g
    step = m * lax.rsqrt(v + 1e-8) + 0.1 * w
    return (w - 0.02 * step).astype(jnp.bfloat16), m, v


def clipped(gradients, sum_of_squares, count):
    factor = jnp.minimum(1.0, 0.5 * lax.rsqrt(sum_of_squares / count + 1e-30))
    return [g * factor for g in gradients]


def stack(weights, h):
    for number in range(weights["w_gate"].shape[0]):
        h = layer(h, {name: w[number] for name, w in weights.items()})
    return h


def solution(mesh):
    groups = mesh.shape["rep"]

    def step(x, dy, *arrays):
        weights, m, v = (arrays[i : i + 3] for i in (0, 3, 6))
        x, dy = (t.reshape(groups, -1, *t.shape[1:]) for t in (x, dy))

        def of_a_group(x, dy):
            _, back = jax.vjp(lambda w: stack(w, x), dict(zip(NAMES, weights, strict=True)))
            by_weights = back(dy)[0]
            gradients = [by_weights[name].astype(jnp.float32) for name in NAMES]
            gradients = clipped(gradients, sum(jnp.sum(g * g) for g in gradients), sum(g.size for g in gradients))
            new = [adamw(w.astype(jnp.float32), m, v, g) for w, m, v, g in zip(weights, m, v, gradients, strict=True)]
            return tuple(one[which] for which in range(3) for one in new)

        return tuple(t.reshape(-1, *t.shape[2:]) for t in jax.vmap(of_a_group)(x, dy))

    return step
```

profile of v0, /device:TPU:0, one launch (start us, length us, event | category | flops | bytes accessed | tf_op | source)
XLA Modules:
  0.0 1973.9 jit_solution(6177760407571660727)
XLA Ops:
  23.2 21.9 %fusion.173 = f32[2048,3072]{1,0:T(8,128)} fusion(bf16[2,1280,3072]{2,1,0:T(8,128)(2,1)} %param.12, bf16[1,2048,1280]{1,2,0:T(8,128)(2,1)S(1)} %fusion.157), kind=kOutput, calls=%fused_computation.224 | convolution fusion | flops 16106127360 | bytes 38273024 | tf_op jit(solution)/vmap(jvp())/dot_general | solution.py:20
  45.1 34.6 %fusion.150 = (bf16[1,2048,3072]{2,1,0:T(8,128)(2,1)}, f32[2048,3072]{1,0:T(8,128)}) fusion(f32[2048,3072]{1,0:T(8,128)} %fusion.173, bf16[2,1280,3072]{2,1,0:T(8,128)(2,1)} %param.17, bf16[1,2048,1280]{1,2,0:T(8,128)(2,1)} %copy-done), kind=kOutput, calls=%fused_computation.189 | convolution fusion | flops 16143876096 | bytes 76021760 | tf_op jit(solution)/vmap(jvp())/dot_general | solution.py:21
  79.7 22.7 %fusion.160 = (f32[2048]{0:T(1024)S(1)}, bf16[1,2048,1280]{1,2,0:T(8,128)(2,1)S(1)}) fusion(bf16[1,2048,1280]{1,2,0:T(8,128)(2,1)} %copy.1, bf16[2,3072,1280]{2,1,0:T(8,128)(2,1)} %param.15, bf16[1,2048,3072]{2,1,0:T(8,128)(2,1)} %get-tuple-element.263), kind=kOutput, calls=%fused_computation.211 | convolution fusion | flops 16119232512 | bytes 30941184 | tf_op jit(solution)/vmap(jvp())/dot_general | solution.py:9
  107.4 22.1 %fusion.166 = f32[2048,3072]{1,0:T(8,128)} fusion(bf16[2,1280,3072]{2,1,0:T(8,128)(2,1)} %param.17, bf16[1,2048,1280]{1,2,0:T(8,128)(2,1)S(1)} %fusion.161), kind=kOutput, calls=%fused_computation.217 | convolution fusion | flops 16106127360 | bytes 38273024 | tf_op jit(solution)/vmap(jvp())/dot_general | solution.py:21
  129.5 22.0 %convolution_convert_fusion.1 = bf16[2048,3072]{1,0:T(8,128)(2,1)} fusion(bf16[2,3072,1280]{2,1,0:T(8,128)(2,1)} %param.15, bf16[1,2048,1280]{2,1,0:T(8,128)(2,1)S(1)} %bitcast.648), kind=kOutput, calls=%fused_computation.206 | convolution fusion | flops 16112418816 | bytes 25690112 | tf_op jit(solution)/vmap(transpose(jvp()))/dot_general | solution.py:9
  151.5 43.7 %fusion.139 = (bf16[1,2048,3072]{2,1,0:T(8,128)(2,1)}, bf16[1,2048,3072]{2,1,0:T(8,128)(2,1)}, f32[2048,3072]{1,0:T(8,128)}) fusion(f32[2048,3072]{1,0:T(8,128)} %fusion.166, bf16[2048,3072]{1,0:T(8,128)(2,1)} %convolution_convert_fusion.1, bf16[2,1280,3072]{2,1,0:T(8,128)(2,1)} %param.12, bf16[1,2048,1280]{1,2,0:T(8,128)(2,1)} %copy-done.1), kind=kOutput, calls=%fused_computation.173 | convolution fusion | flops 16200499200 | bytes 101187584 | tf_op jit(solution)/vmap(jvp())/dot_general | solution.py:20
  195.2 21.6 %fusion.149 = bf16[1,2048,3072]{2,1,0:T(8,128)(2,1)} fusion(f32[2048,3072]{1,0:T(8,128)} %fusion.166, f32[2048,3072]{1,0:T(8,128)} %get-tuple-element.267), kind=kLoop, calls=%fused_computation.187 | loop fusion | flops 37748736 | bytes 62914560 | tf_op jit(solution)/vmap(jvp())/convert_element_type | solution.py:22
  233.7 207.8 %while.16 = (bf16[1,2048,3072]{1,2,0:T(8,128)(2,1)}, bf16[1,2048,1280]{2,1,0:T(8,128)(2,1)}, f32[192,1280]{1,0:T(8,128)S(1)}, f32[192,1280]{1,0:T(8,128)}, u32[]...) while((bf16[1,2048,3072]{1,2,0:T(8,128)(2,1)}, ...), condition=%wide.windowed_dot_general_cond_rs.4.clone, body=%wide.windowed_dot_general_body_rs.4.clone.sunk | while | flops 4034297856 | bytes 71041624 | solution.py:9
  252.7 20.1 %collective-permute-start.18 = (f32[192,1280]{1,0:T(8,128)S(1)}, f32[192,1280]{1,0:T(8,128)S(1)}, u32[]{:S(2)}, u32[]{:S(2)}) collective-permute-start(f32[192,1280]{1,0:T(8,128)S(1)} %get-tuple-element.491), channel_id=31, source_target_pairs={{0,1},{1,2},{2,3},{3,4},{4,5},{5,6},{6,7},{7,8},{8,9},{9,10},{10,1... | collective-permute-start | bytes 2949128 | tf_op jit(solution)/vmap(transpose(jvp()))/dot_general | solution.py:9
  452.9 200.6 %while.14 = (bf16[1,2048,3072]{2,1,0:T(8,128)(2,1)}, bf16[1,2048,1280]{1,2,0:T(8,128)(2,1)}, f32[3072,80]{0,1:T(8,128)S(1)}, f32[3072,80]{0,1:T(8,128)}, u32[]{:...) while((bf16[1,2048,3072]{2,1,0:T(8,128)(2,1)}, ...), condition=%wide.windowed_dot_general_cond_rs.2.clone, body=%wide.windowed_dot_general_body_rs.2.clone.sunk | while | flops 4030627840 | bytes 124519128 | solution.py:21
  470.3 20.1 %collective-permute-start.10 = (f32[3072,80]{0,1:T(8,128)S(1)}, f32[3072,80]{0,1:T(8,128)S(1)}, u32[]{:S(2)}, u32[]{:S(2)}) collective-permute-start(f32[3072,80]{0,1:T(8,128)S(1)} %get-tuple-element.473), channel_id=18, source_target_pairs={{0,1},{1,2},{2,3},{3,4},{4,5},{5,6},{6,7},{7,8},{8,9},{9,10},{10,1... | collective-permute-start | bytes 2949128 | tf_op jit(solution)/vmap(transpose(jvp()))/dot_general | solution.py:21
  665.9 22.7 %fusion.184 = bf16[2048,1280]{0,1:T(8,128)(2,1)} fusion(bf16[1,2048,3072]{2,1,0:T(8,128)(2,1)} %get-tuple-element.743, bf16[2,1280,3072]{2,1,0:T(8,128)(2,1)} %param.17), kind=kOutput, calls=%fused_computation.231 | convolution fusion | flops 16106127360 | bytes 25690112 | tf_op jit(solution)/vmap(transpose(jvp()))/dot_general | solution.py:21
  696.4 25.0 %fusion.162 = (f32[2048]{0:T(1024)S(1)}, bf16[1,2048,1280]{1,2,0:T(8,128)(2,1)}) fusion(bf16[1,2048,1280]{1,2,0:T(8,128)(2,1)} %copy-done.12, bf16[2048,1280]{0,1:T(8,128)(2,1)} %fusion.184, bf16[2,1280,3072]{2,1,0:T(8,128)(2,1)} %param.12, bf16[1,2048,3072]{2,1,0:T(8,128)(2,1)} %get-tuple-element.540), kind=kOutput, calls=%fused_computation.213 | convolution fusion | flops 16119232512 | bytes 36184064 | tf_op jit(solution)/vmap(transpose(jvp()))/dot_general | solution.py:20
  733.8 39.5 %convert_multiply_fusion = (bf16[1,2048,3072]{2,1,0:T(8,128)(2,1)}, bf16[1,2048,3072]{2,1,0:T(8,128)(2,1)}) fusion(f32[2048,3072]{1,0:T(8,128)} %fusion.173, f32[2048,3072]{1,0:T(8,128)} %get-tuple-element.264, bf16[2,3072,1280]{2,1,0:T(8,128)(2,1)} %param.15, bf16[1,2048,1280]{1,2,0:T(8,128)(2,1)} %fusion.220), kind=kOutput, calls=%fused_computation.168 | convolution fusion | flops 16206790656 | bytes 88604672 | tf_op jit(solution)/vmap(transpose(jvp()))/dot_general | solution.py:9
  773.3 194.8 %while.15 = (bf16[1,2048,3072]{2,1,0:T(8,128)(2,1)}, bf16[1,2048,1280]{1,2,0:T(8,128)(2,1)}, f32[3072,80]{0,1:T(8,128)S(1)}, f32[3072,80]{0,1:T(8,128)}, u32[]{:...) while((bf16[1,2048,3072]{2,1,0:T(8,128)(2,1)}, ...), condition=%wide.windowed_dot_general_cond_rs.3.clone, body=%wide.windowed_dot_general_body_rs.3.clone.sunk | while | flops 4030627840 | bytes 124519128 | solution.py:21
  790.0 20.1 %collective-permute-start.14 = (f32[3072,80]{0,1:T(8,128)S(1)}, f32[3072,80]{0,1:T(8,128)S(1)}, u32[]{:S(2)}, u32[]{:S(2)}) collective-permute-start(f32[3072,80]{0,1:T(8,128)S(1)} %get-tuple-element.482), channel_id=24, source_target_pairs={{0,1},{1,2},{2,3},{3,4},{4,5},{5,6},{6,7},{7,8},{8,9},{9,10},{10,1... | collective-permute-start | bytes 2949128 | tf_op jit(solution)/vmap(transpose(jvp()))/dot_general | solution.py:21
  1005.0 214.3 %while.17 = (bf16[1,2048,1280]{2,1,0:T(8,128)(2,1)}, bf16[1,2048,3072]{1,2,0:T(8,128)(2,1)}, f32[1280,192]{0,1:T(8,128)S(1)}, f32[1280,192]{0,1:T(8,128)}, u32[]...) while((bf16[1,2048,1280]{2,1,0:T(8,128)(2,1)}, ...), condition=%wide.windowed_dot_general_cond_rs.5.clone, body=%wide.windowed_dot_general_body_rs.5.clone.sunk | while | flops 4034297856 | bytes 71041624 | solution.py:9
  1024.9 20.0 %collective-permute-start.22 = (f32[1280,192]{0,1:T(8,128)}, f32[1280,192]{0,1:T(8,128)}, u32[]{:S(2)}, u32[]{:S(2)}) collective-permute-start(f32[1280,192]{0,1:T(8,128)} %get-tuple-element.500), channel_id=37, source_target_pairs={{0,1},{1,2},{2,3},{3,4},{4,5},{5,6},{6,7},{7,8},{8,9},{9,10},{10,1... | collective-permute-start | bytes 2949128 | tf_op jit(solution)/vmap(transpose(jvp()))/dot_general | solution.py:9
  1220.2 193.7 %while.12 = (bf16[1,2048,3072]{2,1,0:T(8,128)(2,1)}, bf16[1,2048,1280]{1,2,0:T(8,128)(2,1)}, f32[3072,80]{0,1:T(8,128)S(1)}, f32[3072,80]{0,1:T(8,128)S(1)}, u32...) while((bf16[1,2048,3072]{2,1,0:T(8,128)(2,1)}, ...), condition=%wide.windowed_dot_general_cond_rs.clone, body=%wide.windowed_dot_general_body_rs.clone.sunk | while | flops 4030627840 | bytes 124519128 | solution.py:20
  1414.8 205.7 %while.13 = (bf16[1,2048,3072]{2,1,0:T(8,128)(2,1)}, bf16[1,2048,1280]{1,2,0:T(8,128)(2,1)}, f32[3072,80]{0,1:T(8,128)S(1)}, f32[3072,80]{0,1:T(8,128)}, u32[]{:...) while((bf16[1,2048,3072]{2,1,0:T(8,128)(2,1)}, ...), condition=%wide.windowed_dot_general_cond_rs.1.clone, body=%wide.windowed_dot_general_body_rs.1.clone.sunk | while | flops 4030627840 | bytes 124519128 | solution.py:20
  1662.0 41.7 %all-reduce.10 = f32[]{:T(128)} all-reduce(f32[]{:T(128)S(6)} %add.180), channel_id=13, replica_groups=mesh['rep'=1,'dp'=16] {'dp'}, use_global_device_ids=true, to_apply=%region_3.4.clone | all-reduce | flops 1 | bytes 8 | tf_op jit(solution)/vmap()/reduce_sum | solution.py:54
  1722.3 61.9 %all-gather.14.cloned.1.call-done = bf16[1,2,3072,1280]{3,2,1,0:T(8,128)(2,1)} async-done(((bf16[1,2,192,1280]{3,2,1,0:T(8,128)(2,1)}), bf16[1,2,3072,1280]{3,2,1,0:T(8,128)(2,1)}) %all-gather.14.cloned.1.call-update) | async-done | bytes 15728656 | tf_op jit(solution)/reshape | solution.py:58
  1784.2 75.4 %all-gather.12.cloned.1.call-done = bf16[1,2,1280,3072]{3,2,1,0:T(8,128)(2,1)} async-done(((bf16[1,2,80,3072]{3,2,1,0:T(8,128)(2,1)}), bf16[1,2,1280,3072]{3,2,1,0:T(8,128)(2,1)}) %all-gather.12.cloned.1.call-update) | async-done | bytes 15728656 | tf_op jit(solution)/reshape | solution.py:58
  1859.6 75.4 %all-gather.10.cloned.1.call-done = bf16[1,2,1280,3072]{3,2,1,0:T(8,128)(2,1)} async-done(((bf16[1,2,80,3072]{3,2,1,0:T(8,128)(2,1)}), bf16[1,2,1280,3072]{3,2,1,0:T(8,128)(2,1)}) %all-gather.10.cloned.1.call-update) | async-done | bytes 15728656 | tf_op jit(solution)/reshape | solution.py:58
  (640 shorter events, 1344.0 us)
Async XLA Ops:
  7.2 1777.0 %all-gather.14.cloned.1.call-start = ((), (), s32[]{:S(2)}) async-start(), calls=%async_computation.2 | async-start | bytes 16711680 | tf_op jit(solution)/reshape | solution.py:58
  252.7 25.2 %collective-permute-start.18 = (f32[192,1280]{1,0:T(8,128)S(1)}, f32[192,1280]{1,0:T(8,128)S(1)}, u32[]{:S(2)}, u32[]{:S(2)}) collective-permute-start(f32[192,1280]{1,0:T(8,128)S(1)} %get-tuple-element.491), channel_id=31, source_target_pairs={{0,1},{1,2},{2,3},{3,4},{4,5},{5,6},{6,7},{7,8},{8,9},{9,10},{10,1... | collective-permute-start | bytes 2949128 | tf_op jit(solution)/vmap(transpose(jvp()))/dot_general | solution.py:9
  441.4 1197.4 %collective-permute-start.28 = (f32[192,1280]{1,0:T(8,128)}, f32[192,1280]{1,0:T(8,128)}, u32[]{:S(2)}, u32[]{:S(2)}) collective-permute-start(f32[192,1280]{1,0:T(8,128)} %get-tuple-element.45), channel_id=32, source_target_pairs={{0,1},{1,2},{2,3},{3,4},{4,5},{5,6},{6,7},{7,8},{8,9},{9,10},{10,1... | collective-permute-start | bytes 2949128 | tf_op jit(solution)/vmap(transpose(jvp()))/dot_general | solution.py:9
  470.3 22.5 %collective-permute-start.10 = (f32[3072,80]{0,1:T(8,128)S(1)}, f32[3072,80]{0,1:T(8,128)S(1)}, u32[]{:S(2)}, u32[]{:S(2)}) collective-permute-start(f32[3072,80]{0,1:T(8,128)S(1)} %get-tuple-element.473), channel_id=18, source_target_pairs={{0,1},{1,2},{2,3},{3,4},{4,5},{5,6},{6,7},{7,8},{8,9},{9,10},{10,1... | collective-permute-start | bytes 2949128 | tf_op jit(solution)/vmap(transpose(jvp()))/dot_general | solution.py:21
  554.5 20.6 %collective-permute-start.8 = (f32[3072,80]{0,1:T(8,128)}, f32[3072,80]{0,1:T(8,128)S(1)}, u32[]{:S(2)}, u32[]{:S(2)}) collective-permute-start(f32[3072,80]{0,1:T(8,128)} %broadcast_select_fusion.28), channel_id=16, source_target_pairs={{0,1},{1,2},{2,3},{3,4},{4,5},{5,6},{6,7},{7,8},{8,9},{9,10},{10,1... | collective-permute-start | bytes 2949128 | tf_op jit(solution)/vmap(transpose(jvp()))/dot_general | solution.py:21
  604.8 20.6 %collective-permute-start.8 = (f32[3072,80]{0,1:T(8,128)}, f32[3072,80]{0,1:T(8,128)S(1)}, u32[]{:S(2)}, u32[]{:S(2)}) collective-permute-start(f32[3072,80]{0,1:T(8,128)} %broadcast_select_fusion.28), channel_id=16, source_target_pairs={{0,1},{1,2},{2,3},{3,4},{4,5},{5,6},{6,7},{7,8},{8,9},{9,10},{10,1... | collective-permute-start | bytes 2949128 | tf_op jit(solution)/vmap(transpose(jvp()))/dot_general | solution.py:21
  653.4 982.1 %collective-permute-start.26 = (f32[3072,80]{0,1:T(8,128)}, f32[3072,80]{0,1:T(8,128)}, u32[]{:S(2)}, u32[]{:S(2)}) collective-permute-start(f32[3072,80]{0,1:T(8,128)} %get-tuple-element.41), channel_id=19, source_target_pairs={{0,1},{1,2},{2,3},{3,4},{4,5},{5,6},{6,7},{7,8},{8,9},{9,10},{10,1... | collective-permute-start | bytes 2949128 | tf_op jit(solution)/vmap(transpose(jvp()))/dot_general | solution.py:21
  790.0 22.3 %collective-permute-start.14 = (f32[3072,80]{0,1:T(8,128)S(1)}, f32[3072,80]{0,1:T(8,128)S(1)}, u32[]{:S(2)}, u32[]{:S(2)}) collective-permute-start(f32[3072,80]{0,1:T(8,128)S(1)} %get-tuple-element.482), channel_id=24, source_target_pairs={{0,1},{1,2},{2,3},{3,4},{4,5},{5,6},{6,7},{7,8},{8,9},{9,10},{10,1... | collective-permute-start | bytes 2949128 | tf_op jit(solution)/vmap(transpose(jvp()))/dot_general | solution.py:21
  870.1 20.7 %collective-permute-start.12 = (f32[3072,80]{0,1:T(8,128)S(1)}, f32[3072,80]{0,1:T(8,128)S(1)}, u32[]{:S(2)}, u32[]{:S(2)}) collective-permute-start(f32[3072,80]{0,1:T(8,128)S(1)} %broadcast_select_fusion.30), channel_id=22, source_target_pairs={{0,1},{1,2},{2,3},{3,4},{4,5},{5,6},{6,7},{7,8},{8,9},{9,10},{10,1... | collective-permute-start | bytes 2949128 | tf_op jit(solution)/vmap(transpose(jvp()))/dot_general | solution.py:21
  919.9 20.7 %collective-permute-start.12 = (f32[3072,80]{0,1:T(8,128)S(1)}, f32[3072,80]{0,1:T(8,128)S(1)}, u32[]{:S(2)}, u32[]{:S(2)}) collective-permute-start(f32[3072,80]{0,1:T(8,128)S(1)} %broadcast_select_fusion.30), channel_id=22, source_target_pairs={{0,1},{1,2},{2,3},{3,4},{4,5},{5,6},{6,7},{7,8},{8,9},{9,10},{10,1... | collective-permute-start | bytes 2949128 | tf_op jit(solution)/vmap(transpose(jvp()))/dot_general | solution.py:21
  968.0 669.1 %collective-permute-start.27 = (f32[3072,80]{0,1:T(8,128)}, f32[3072,80]{0,1:T(8,128)}, u32[]{:S(2)}, u32[]{:S(2)}) collective-permute-start(f32[3072,80]{0,1:T(8,128)} %get-tuple-element.43), channel_id=25, source_target_pairs={{0,1},{1,2},{2,3},{3,4},{4,5},{5,6},{6,7},{7,8},{8,9},{9,10},{10,1... | collective-permute-start | bytes 2949128 | tf_op jit(solution)/vmap(transpose(jvp()))/dot_general | solution.py:21
  1024.9 25.2 %collective-permute-start.22 = (f32[1280,192]{0,1:T(8,128)}, f32[1280,192]{0,1:T(8,128)}, u32[]{:S(2)}, u32[]{:S(2)}) collective-permute-start(f32[1280,192]{0,1:T(8,128)} %get-tuple-element.500), channel_id=37, source_target_pairs={{0,1},{1,2},{2,3},{3,4},{4,5},{5,6},{6,7},{7,8},{8,9},{9,10},{10,1... | collective-permute-start | bytes 2949128 | tf_op jit(solution)/vmap(transpose(jvp()))/dot_general | solution.py:9
  1221.4 19.6 collective-permute-start
  1269.6 20.6 %collective-permute-start = (f32[3072,80]{0,1:T(8,128)}, f32[3072,80]{0,1:T(8,128)S(1)}, u32[]{:S(2)}, u32[]{:S(2)}) collective-permute-start(f32[3072,80]{0,1:T(8,128)} %broadcast_select_fusion.24), channel_id=3, source_target_pairs={{0,1},{1,2},{2,3},{3,4},{4,5},{5,6},{6,7},{7,8},{8,9},{9,10},{10,1... | collective-permute-start | bytes 2949128 | tf_op jit(solution)/vmap(transpose(jvp()))/dot_general | solution.py:20
  1318.2 20.6 %collective-permute-start = (f32[3072,80]{0,1:T(8,128)}, f32[3072,80]{0,1:T(8,128)S(1)}, u32[]{:S(2)}, u32[]{:S(2)}) collective-permute-start(f32[3072,80]{0,1:T(8,128)} %broadcast_select_fusion.24), channel_id=3, source_target_pairs={{0,1},{1,2},{2,3},{3,4},{4,5},{5,6},{6,7},{7,8},{8,9},{9,10},{10,1... | collective-permute-start | bytes 2949128 | tf_op jit(solution)/vmap(transpose(jvp()))/dot_general | solution.py:20
  1366.3 20.6 %collective-permute-start = (f32[3072,80]{0,1:T(8,128)}, f32[3072,80]{0,1:T(8,128)S(1)}, u32[]{:S(2)}, u32[]{:S(2)}) collective-permute-start(f32[3072,80]{0,1:T(8,128)} %broadcast_select_fusion.24), channel_id=3, source_target_pairs={{0,1},{1,2},{2,3},{3,4},{4,5},{5,6},{6,7},{7,8},{8,9},{9,10},{10,1... | collective-permute-start | bytes 2949128 | tf_op jit(solution)/vmap(transpose(jvp()))/dot_general | solution.py:20
  1415.9 20.6 %collective-permute-start.4 = (f32[3072,80]{0,1:T(8,128)}, f32[3072,80]{0,1:T(8,128)}, u32[]{:S(2)}, u32[]{:S(2)}) collective-permute-start(f32[3072,80]{0,1:T(8,128)} %broadcast_select_fusion.26), channel_id=9, source_target_pairs={{0,1},{1,2},{2,3},{3,4},{4,5},{5,6},{6,7},{7,8},{8,9},{9,10},{10,1... | collective-permute-start | bytes 2949128 | tf_op jit(solution)/vmap(transpose(jvp()))/dot_general | solution.py:20
  1467.4 20.6 %collective-permute-start.4 = (f32[3072,80]{0,1:T(8,128)}, f32[3072,80]{0,1:T(8,128)}, u32[]{:S(2)}, u32[]{:S(2)}) collective-permute-start(f32[3072,80]{0,1:T(8,128)} %broadcast_select_fusion.26), channel_id=9, source_target_pairs={{0,1},{1,2},{2,3},{3,4},{4,5},{5,6},{6,7},{7,8},{8,9},{9,10},{10,1... | collective-permute-start | bytes 2949128 | tf_op jit(solution)/vmap(transpose(jvp()))/dot_general | solution.py:20
  1519.3 20.6 %collective-permute-start.4 = (f32[3072,80]{0,1:T(8,128)}, f32[3072,80]{0,1:T(8,128)}, u32[]{:S(2)}, u32[]{:S(2)}) collective-permute-start(f32[3072,80]{0,1:T(8,128)} %broadcast_select_fusion.26), channel_id=9, source_target_pairs={{0,1},{1,2},{2,3},{3,4},{4,5},{5,6},{6,7},{7,8},{8,9},{9,10},{10,1... | collective-permute-start | bytes 2949128 | tf_op jit(solution)/vmap(transpose(jvp()))/dot_general | solution.py:20
  1570.8 20.6 %collective-permute-start.4 = (f32[3072,80]{0,1:T(8,128)}, f32[3072,80]{0,1:T(8,128)}, u32[]{:S(2)}, u32[]{:S(2)}) collective-permute-start(f32[3072,80]{0,1:T(8,128)} %broadcast_select_fusion.26), channel_id=9, source_target_pairs={{0,1},{1,2},{2,3},{3,4},{4,5},{5,6},{6,7},{7,8},{8,9},{9,10},{10,1... | collective-permute-start | bytes 2949128 | tf_op jit(solution)/vmap(transpose(jvp()))/dot_general | solution.py:20
  1620.6 19.7 collective-permute-start.29
  1635.5 23.3 %collective-permute-start.25 = (f32[3072,80]{0,1:T(8,128)}, f32[3072,80]{0,1:T(8,128)S(1)}, u32[]{:S(2)}, u32[]{:S(2)}) collective-permute-start(f32[3072,80]{0,1:T(8,128)} %get-tuple-element.39), channel_id=12, source_target_pairs={{0,1},{1,2},{2,3},{3,4},{4,5},{5,6},{6,7},{7,8},{8,9},{9,10},{10,1... | collective-permute-start | bytes 2949128 | tf_op jit(solution)/vmap(transpose(jvp()))/dot_general | solution.py:20
  1710.6 149.0 %all-gather.12.cloned.1.call-start = ((), (), s32[]{:S(2)}) async-start(), calls=%async_computation.1 | async-start | bytes 16711680 | tf_op jit(solution)/reshape | solution.py:58
  1716.5 218.5 %all-gather.10.cloned.1.call-start = ((), (), s32[]{:S(2)}) async-start(), calls=%async_computation | async-start | bytes 16711680 | tf_op jit(solution)/reshape | solution.py:58
  (189 other events, 3543.5 us)
Sparse Core Ops, SparseCore 0:
  1710.7 73.3 all-gather.13
  1787.0 72.5 all-gather.11
  1862.4 72.5 all-gather.9
where the time goes:
time: 1980 us; the launch traced here: 1970 us
  starting transfers between devices  590 us (30%)
  waiting for transfers between devices  551 us (28%)
  matrix products  487 us (25%)
  other arithmetic  187 us (9%)
  local copies, waits for them, and re-layouts  97.4 us (5%)
  blocking collectives  41.7 us (2%)
    reshape x3, waiting for transfers between devices, step(): t.reshape(-1, *t.shape[2:])  213 us
    dot_general x34, starting transfers between devices, matmul(): jnp.dot(a, w, preferred_element_type=jnp.float32).astype(jnp.bfloat16)  203 us
    dot_general x34, starting transfers between devices, layer(): up = jnp.dot(a, w['w_up'], preferred_element_type=jnp.float32)  203 us
    dot_general x34, starting transfers between devices, layer(): gate = jnp.dot(a, w['w_gate'], preferred_element_type=jnp.float32)  184 us
    dot_general x19, matrix products, matmul(): jnp.dot(a, w, preferred_element_type=jnp.float32).astype(jnp.bfloat16)  167 us
    dot_general x19, matrix products, layer(): gate = jnp.dot(a, w['w_gate'], preferred_element_type=jnp.float32)  165 us
    dot_general x19, matrix products, layer(): up = jnp.dot(a, w['w_up'], preferred_element_type=jnp.float32)  155 us
    dot_general x34, waiting for transfers between devices, layer(): gate = jnp.dot(a, w['w_gate'], preferred_element_type=jnp.float32)  125 us
  transfers between devices with their start and end apart: 105, of which 72 were waited for; matrix products, arithmetic and copies ran while one was open for 25% of the time, Pallas kernels for 0%

commit v1 on v0

v1 whole, which is shorter than its diff:
```python
import jax
import jax.numpy as jnp
from jax import lax
from jax.sharding import PartitionSpec as P

F32, BF16 = jnp.float32, jnp.bfloat16


def dot(a, b, contract):
    return lax.dot_general(a, b, ((contract[:1], contract[1:]), ((), ())), preferred_element_type=F32)


def normed(h):
    wide = h.astype(F32)
    scale = lax.rsqrt(jnp.mean(wide**2, -1, keepdims=True) + 1e-6)
    return (wide * scale).astype(BF16), wide, scale


def gated(gate, up):
    return (jax.nn.silu(gate) * up).astype(BF16)


def gated_back(gate, up, d):
    d = d.astype(F32)
    s = jax.nn.sigmoid(gate)
    return (d * up * (s * (1 + gate * (1 - s)))).astype(BF16), (d * (gate * s)).astype(BF16)


def adamw(w, m, v, g):
    m = 0.9 * m + 0.1 * g
    v = 0.95 * v + 0.05 * g * g
    step = m * lax.rsqrt(v + 1e-8) + 0.1 * w
    return (w - 0.02 * step).astype(BF16), m, v


def solution(mesh):
    n = mesh.shape["dp"]

    def step(x, dy, wg, wu, wd, *moments):
        x, dy = x[0], dy[0]
        scatter = lambda g: lax.psum_scatter(g.astype(BF16), "dp", scatter_dimension=0, tiled=True)
        a0, _, _ = normed(x)
        gate0, up0 = dot(a0, wg[0], (1, 0)), dot(a0, wu[0], (1, 0))
        hid0 = gated(gate0, up0)
        h1 = x + dot(hid0, wd[0], (1, 0)).astype(BF16)
        a1, wide1, scale1 = normed(h1)
        gate1, up1 = dot(a1, wg[1], (1, 0)), dot(a1, wu[1], (1, 0))
        hid1 = gated(gate1, up1)
        gd1 = scatter(dot(hid1, dy, (0, 0)))
        dgate1, dup1 = gated_back(gate1, up1, dot(dy, wd[1], (1, 1)).astype(BF16))
        gg1 = scatter(dot(a1, dgate1, (0, 0)))
        gu1 = scatter(dot(a1, dup1, (0, 0)))
        da = dot(dgate1, wg[1], (1, 1)).astype(BF16) + dot(dup1, wu[1], (1, 1)).astype(BF16)
        da = da.astype(F32)
        dwide = scale1 * da - wide1 * (scale1**3 * jnp.mean(da * wide1, -1, keepdims=True))
        dh = dy + dwide.astype(BF16)
        gd0 = scatter(dot(hid0, dh, (0, 0)))
        dgate0, dup0 = gated_back(gate0, up0, dot(dh, wd[0], (1, 1)).astype(BF16))
        gg0 = scatter(dot(a0, dgate0, (0, 0)))
        gu0 = scatter(dot(a0, dup0, (0, 0)))
        grads = [[g.astype(F32) for g in pair] for pair in ((gg0, gg1), (gu0, gu1), (gd0, gd1))]
        total = lax.psum(sum(jnp.sum(g * g) for pair in grads for g in pair), "dp")
        count = wg.size + wu.size + wd.size
        factor = jnp.minimum(1.0, 0.5 * lax.rsqrt(total / count + 1e-30))
        me = lax.axis_index("dp")
        new_w, new_m, new_v = [], [], []
        for w, m, v, pair in zip((wg, wu, wd), moments[:3], moments[3:], grads):
            rows = w.shape[1] // n
            full, ms, vs = [], [], []
            for l in range(2):
                mine = lax.dynamic_slice_in_dim(w[l], me * rows, rows, 0)
                nw, nm, nv = adamw(mine.astype(F32), m[l], v[l], pair[l] * factor)
                full.append(lax.all_gather(nw, "dp", axis=0, tiled=True))
                ms.append(nm)
                vs.append(nv)
            new_w.append(jnp.stack(full))
            new_m.append(jnp.stack(ms))
            new_v.append(jnp.stack(vs))
        return (*new_w, *new_m, *new_v)

    whole, rows = P(None, None, None), P(None, "dp", None)
    outs = (P("rep", None, None),) * 3 + (P("rep", "dp", None),) * 6
    return jax.shard_map(
        step, mesh=mesh, in_specs=(P(("rep", "dp"), None, None),) * 2 + (whole,) * 3 + (rows,) * 6, out_specs=outs, check_vma=False
    )
```

time: 1980 us -> 1080 us (0.55)
  starting transfers between devices: 590 us -> 0.49 us
  matrix products: 487 us -> 387 us
  other arithmetic: 187 us -> 87.7 us
  local copies, waits for them, and re-layouts: 97.4 us -> 41.4 us
  waiting for transfers between devices: 551 us -> 501 us
    dot_general x102 -> x0, starting transfers between devices: 590 us -> none  [the longest x34 203 us: matmul(): jnp.dot(a, w, preferred_element_type=jnp.float32).astype(jnp.bfloat16)]
    dot_general x102 -> x0, waiting for transfers between devices: 338 us -> none  [the longest x34 125 us: layer(): gate = jnp.dot(a, w['w_gate'], preferred_element_type=jnp.float32)]
    reduce_scatter x0 -> x6, waiting for transfers between devices: none -> 264 us  [step(): lax.psum_scatter(g.astype(BF16), 'dp', scatter_dimension=0, tiled=True)]
    all_gather x0 -> x6, waiting for transfers between devices: none -> 235 us  [step(): full.append(lax.all_gather(nw, 'dp', axis=0, tiled=True))]
    reshape x3 -> x0, waiting for transfers between devices: 213 us -> none  [step(): t.reshape(-1, *t.shape[2:])]
    dot_general x128 -> x0, other arithmetic: 119 us -> none
    dot_general x57 -> x15, matrix products: 487 us -> 387 us  [dot(): lax.dot_general(a, b, ((contract[:1], contract[1:]), ((), ())), preferred...]
    unnamed x64 -> x56, local copies, waits for them, and re-layouts: 97 us -> 16.2 us
  transfers between devices with their start and end apart: 105 -> 12, of which waited for: 72 -> 10; matrix products, arithmetic and copies ran while one was open for 25% -> 28% of each run, Pallas kernels for 0% -> 0%
where the time goes in v1:
time: 1080 us; the launch traced here: 1070 us
  waiting for transfers between devices  501 us (46%)
  matrix products  387 us (36%)
  other arithmetic  87.7 us (8%)
  local copies, waits for them, and re-layouts  41.4 us (4%)
  blocking collectives  31.8 us (3%)
  between operations  19.6 us (2%)
    dot_general x15, matrix products, dot(): lax.dot_general(a, b, ((contract[:1], contract[1:]), ((), ())), preferred...  387 us
    reduce_scatter x6, waiting for transfers between devices, step(): lax.psum_scatter(g.astype(BF16), 'dp', scatter_dimension=0, tiled=True)  264 us
    all_gather x6, waiting for transfers between devices, step(): full.append(lax.all_gather(nw, 'dp', axis=0, tiled=True))  235 us
    another operation x3, other arithmetic, step(): new_w.append(jnp.stack(full))  39.6 us
    psum x1, blocking collectives, step(): lax.psum(sum((jnp.sum(g * g) for pair in grads for g in pair)), 'dp')  31.8 us
  transfers between devices with their start and end apart: 12, of which 10 were waited for; matrix products, arithmetic and copies ran while one was open for 28% of the time, Pallas kernels for 0%

profile of v1, /device:TPU:0, one launch (start us, length us, event | category | flops | bytes accessed | tf_op | source)
XLA Modules:
  0.0 1069.1 jit_solution(1547605708286685144)
XLA Ops:
  18.8 23.2 %fusion.41 = f32[2048,3072]{1,0:T(8,128)} fusion(bf16[1,2048,1280]{2,1,0:T(8,128)(2,1)} %param.11, f32[2048]{0:T(1024)S(1)} %add_rsqrt_fusion.1, bf16[2,1280,3072]{2,1,0:T(8,128)(2,1)} %param.13), kind=kOutput, calls=%fused_computation.59 | convolution fusion | flops 16113991680 | bytes 38281216 | tf_op jit(solution)/shard_map/dot_general | solution.py:10
  42.0 34.9 %multiply_convert_fusion.1 = (bf16[2048,3072]{1,0:T(8,128)(2,1)}, f32[2048,3072]{1,0:T(8,128)}) fusion(f32[2048,3072]{1,0:T(8,128)} %fusion.41, bf16[2,1280,3072]{2,1,0:T(8,128)(2,1)} %param.14, bf16[1,2048,1280]{2,1,0:T(8,128)(2,1)} %param.11, f32[2048]{0:T(1024)S(1)} %add_rsqrt_fusion.1), kind=kOutput, calls=%fused_computation.13 | convolution fusion | flops 16151740416 | bytes 76029952 | tf_op jit(solution)/shard_map/dot_general | solution.py:10
  76.9 24.0 %fusion.24 = (f32[2048]{0:T(1024)S(1)}, bf16[2048,1280]{0,1:T(8,128)(2,1)}) fusion(bf16[2048,3072]{1,0:T(8,128)(2,1)} %get-tuple-element.35, bf16[2,3072,1280]{2,1,0:T(8,128)(2,1)} %param.15, bf16[1,2048,1280]{1,2,0:T(8,128)(2,1)} %copy.20), kind=kOutput, calls=%fused_computation.41 | convolution fusion | flops 16119232512 | bytes 30941184 | tf_op jit(solution)/shard_map/dot_general | solution.py:10
  100.9 22.4 %convolution_convert_fusion.4 = bf16[2048,3072]{1,0:T(8,128)(2,1)} fusion(bf16[1,2048,1280]{2,1,0:T(8,128)(2,1)} %param.12, bf16[2,3072,1280]{2,1,0:T(8,128)(2,1)} %param.15), kind=kOutput, calls=%fused_computation.35 | convolution fusion | flops 16112418816 | bytes 25690112 | tf_op jit(solution)/shard_map/dot_general | solution.py:10
  144.0 42.6 %fusion.1 = (bf16[2048,3072]{1,0:T(8,128)(2,1)}, bf16[2048,3072]{1,0:T(8,128)(2,1)}, f32[2048,3072]{1,0:T(8,128)}) fusion(bf16[2048,3072]{1,0:T(8,128)(2,1)} %convolution_convert_fusion.4, f32[2048,3072]{1,0:T(8,128)} %fusion.29, bf16[2,1280,3072]{2,1,0:T(8,128)(2,1)} %param.14, bf16[2048,1280]{0,1:T(8,128)(2,1)} %get-tuple-element.38, ...), kind=kOutput, calls=%fused_computation.5 | convolution fusion | flops 16202072064 | bytes 101195776 | tf_op jit(solution)/shard_map/dot_general | solution.py:10
  186.6 22.4 %convolution_convert_fusion.2 = bf16[1280,3072]{1,0:T(8,128)(2,1)} fusion(bf16[2048,3072]{1,0:T(8,128)(2,1)} %get-tuple-element.9, bf16[2048,1280]{0,1:T(8,128)(2,1)} %get-tuple-element.38, f32[2048]{0:T(1024)S(1)} %add_rsqrt_fusion), kind=kOutput, calls=%fused_computation.33 | convolution fusion | flops 16117923840 | bytes 25698304 | tf_op jit(solution)/shard_map/dot_general | solution.py:10
  217.2 22.6 %fusion.46 = bf16[2048,1280]{0,1:T(8,128)(2,1)} fusion(bf16[2048,3072]{1,0:T(8,128)(2,1)} %get-tuple-element.10, bf16[2,1280,3072]{2,1,0:T(8,128)(2,1)} %param.14), kind=kOutput, calls=%fused_computation.62 | convolution fusion | flops 16108748800 | bytes 25690112 | tf_op jit(solution)/shard_map/dot_general | solution.py:10
  239.9 22.1 %fusion.26 = (f32[2048]{0:T(1024)S(1)}, bf16[2048,1280]{0,1:T(8,128)(2,1)}) fusion(bf16[2048,1280]{0,1:T(8,128)(2,1)} %get-tuple-element.38, bf16[2048,1280]{0,1:T(8,128)(2,1)} %fusion.46, bf16[2048,3072]{1,0:T(8,128)(2,1)} %get-tuple-element.9, bf16[2,1280,3072]{2,1,0:T(8,128)(2,1)S(1)} %bitcast.193), kind=kOutput, calls=%fused_computation.43 | convolution fusion | flops 16121853952 | bytes 36184064 | tf_op jit(solution)/shard_map/dot_general | solution.py:10
  274.4 22.4 %convolution_convert_fusion.3 = bf16[2048,3072]{1,0:T(8,128)(2,1)} fusion(bf16[2048,1280]{0,1:T(8,128)(2,1)} %fusion.59, bf16[2,3072,1280]{2,1,0:T(8,128)(2,1)} %param.15), kind=kOutput, calls=%fused_computation.34 | convolution fusion | flops 16112418816 | bytes 25690112 | tf_op jit(solution)/shard_map/dot_general | solution.py:10
  296.8 31.4 %fusion.17 = bf16[1280,3072]{1,0:T(8,128)(2,1)} fusion(f32[2048,3072]{1,0:T(8,128)} %get-tuple-element.36, bf16[2048,3072]{1,0:T(8,128)(2,1)} %convolution_convert_fusion.3, f32[2048,3072]{1,0:T(8,128)} %fusion.41, bf16[1,2048,1280]{1,2,0:T(8,128)(2,1)} %copy.20, f32[2048]{0:T(1024)S(1)} %copy-done.18), kind=kOutput, calls=%fused_computation.36 | convolution fusion | flops 16187129856 | bytes 76029952 | tf_op jit(solution)/shard_map/dot_general | solution.py:10
  328.3 25.0 %fusion.13 = bf16[1280,3072]{1,0:T(8,128)(2,1)} fusion(bf16[2048,3072]{1,0:T(8,128)(2,1)} %convolution_convert_fusion.3, bf16[1,2048,1280]{1,2,0:T(8,128)(2,1)} %copy.20, f32[2048]{0:T(1024)S(1)} %copy-done.18, f32[2048,3072]{1,0:T(8,128)} %fusion.41), kind=kOutput, calls=%fused_computation.30 | convolution fusion | flops 16161964032 | bytes 50864128 | tf_op jit(solution)/shard_map/dot_general | solution.py:10
  353.4 22.3 %convolution_convert_fusion.1 = bf16[1280,3072]{1,0:T(8,128)(2,1)} fusion(bf16[2048,3072]{1,0:T(8,128)(2,1)} %get-tuple-element.10, bf16[2048,1280]{0,1:T(8,128)(2,1)} %get-tuple-element.38, f32[2048]{0:T(1024)S(1)} %copy-done.14), kind=kOutput, calls=%fused_computation.32 | convolution fusion | flops 16117923840 | bytes 25698304 | tf_op jit(solution)/shard_map/dot_general | solution.py:10
  375.8 22.4 %convolution_convert_fusion = bf16[3072,1280]{1,0:T(8,128)(2,1)} fusion(bf16[2048,3072]{1,0:T(8,128)(2,1)} %get-tuple-element.35, bf16[2048,1280]{0,1:T(8,128)(2,1)} %fusion.59), kind=kOutput, calls=%fused_computation.29 | convolution fusion | flops 16110059520 | bytes 25690112 | tf_op jit(solution)/shard_map/dot_general | solution.py:10
  398.2 28.7 %fusion.16 = bf16[3072,1280]{1,0:T(8,128)(2,1)} fusion(f32[2048,3072]{1,0:T(8,128)} %get-tuple-element.39, bf16[1,2048,1280]{2,1,0:T(8,128)(2,1)} %param.12, f32[2048,3072]{1,0:T(8,128)} %fusion.29), kind=kOutput, calls=%fused_computation.31 | convolution fusion | flops 16147808256 | bytes 63438848 | tf_op jit(solution)/shard_map/dot_general | solution.py:10
  443.1 38.5 %reduce-scatter.11.cloned.1.call-done = bf16[80,3072]{1,0:T(8,128)(2,1)} async-done(((bf16[1280,3072]{1,0:T(8,128)(2,1)}), bf16[80,3072]{1,0:T(8,128)(2,1)}) %reduce-scatter.11.cloned.1.call-update) | async-done | bytes 491536 | tf_op jit(solution)/shard_map/reduce_scatter | solution.py:41
  484.2 75.3 %reduce-scatter.13.cloned.1.call-done = bf16[80,3072]{1,0:T(8,128)(2,1)} async-done(((bf16[1280,3072]{1,0:T(8,128)(2,1)}), bf16[80,3072]{1,0:T(8,128)(2,1)}) %reduce-scatter.13.cloned.1.call-update) | async-done | bytes 491536 | tf_op jit(solution)/shard_map/reduce_scatter | solution.py:41
  562.0 75.3 %reduce-scatter.15.cloned.1.call-done = bf16[192,1280]{1,0:T(8,128)(2,1)} async-done(((bf16[3072,1280]{1,0:T(8,128)(2,1)}), bf16[192,1280]{1,0:T(8,128)(2,1)}) %reduce-scatter.15.cloned.1.call-update) | async-done | bytes 491536 | tf_op jit(solution)/shard_map/reduce_scatter | solution.py:41
  639.8 75.3 %reduce-scatter.17.cloned.1.call-done = bf16[192,1280]{1,0:T(8,128)(2,1)} async-done(((bf16[3072,1280]{1,0:T(8,128)(2,1)}), bf16[192,1280]{1,0:T(8,128)(2,1)}) %reduce-scatter.17.cloned.1.call-update) | async-done | bytes 491536 | tf_op jit(solution)/shard_map/reduce_scatter | solution.py:41
  717.7 31.8 %psum.7 = f32[]{:T(128)} all-reduce(f32[]{:T(128)S(6)} %add.171), channel_id=1, replica_groups=mesh['rep'=1,'dp'=16] {'dp'}, use_global_device_ids=true, to_apply=%region_15.16 | all-reduce | flops 1 | bytes 8 | tf_op jit(solution)/shard_map/psum | solution.py:62
  803.0 49.2 %all-gather.17.cloned.1.call-done = bf16[3072,1280]{1,0:T(8,128)(2,1)} async-done(((bf16[192,1280]{1,0:T(8,128)(2,1)}), bf16[3072,1280]{1,0:T(8,128)(2,1)}) %all-gather.17.cloned.1.call-update) | async-done | bytes 7864336 | tf_op jit(solution)/shard_map/all_gather | solution.py:73
  865.4 36.0 %all-gather.11.cloned.1.call-done = bf16[1280,3072]{1,0:T(8,128)(2,1)} async-done(((bf16[80,3072]{1,0:T(8,128)(2,1)}), bf16[1280,3072]{1,0:T(8,128)(2,1)}) %all-gather.11.cloned.1.call-update) | async-done | bytes 7864336 | tf_op jit(solution)/shard_map/all_gather | solution.py:73
  901.4 49.0 %all-gather.13.cloned.1.call-done = bf16[1280,3072]{1,0:T(8,128)(2,1)} async-done(((bf16[80,3072]{1,0:T(8,128)(2,1)}), bf16[1280,3072]{1,0:T(8,128)(2,1)}) %all-gather.13.cloned.1.call-update) | async-done | bytes 7864336 | tf_op jit(solution)/shard_map/all_gather | solution.py:73
  963.6 36.0 %all-gather.7.cloned.1.call-done = bf16[1280,3072]{1,0:T(8,128)(2,1)} async-done(((bf16[80,3072]{1,0:T(8,128)(2,1)}), bf16[1280,3072]{1,0:T(8,128)(2,1)}) %all-gather.7.cloned.1.call-update) | async-done | bytes 7864336 | tf_op jit(solution)/shard_map/all_gather | solution.py:73
  999.6 49.0 %all-gather.9.cloned.1.call-done = bf16[1280,3072]{1,0:T(8,128)(2,1)} async-done(((bf16[80,3072]{1,0:T(8,128)(2,1)}), bf16[1280,3072]{1,0:T(8,128)(2,1)}) %all-gather.9.cloned.1.call-update) | async-done | bytes 7864336 | tf_op jit(solution)/shard_map/all_gather | solution.py:73
  (109 shorter events, 167.6 us)
Async XLA Ops:
  7.2 430.8 %reduce-scatter.9.cloned.1.call-start = ((), (), s32[]{:S(2)}) async-start(), calls=%async_computation.7 | async-start | bytes 8355840 | tf_op jit(solution)/shard_map/reduce_scatter | solution.py:41
  18.8 23.2 %copy-start.17 = (f32[2048]{0:T(1024)}, f32[2048]{0:T(1024)S(1)}, u32[]{:S(2)}) copy-start(f32[2048]{0:T(1024)S(1)} %add_rsqrt_fusion.1) | copy-start | bytes 24580
  76.8 46.5 %slice-start = ((s8[15728640]{0:T(1024)(128)(4,1)}), s8[3145728]{0:T(1024)(128)(4,1)S(1)}, s32[]{:S(2)}) async-start(s8[15728640]{0:T(1024)(128)(4,1)} %bitcast.190), calls=%async_computation.18 | async-start | bytes 6291456
  76.8 46.5 %slice-start.1 = ((s8[15728640]{0:T(1024)(128)(4,1)}), s8[4194304]{0:T(1024)(128)(4,1)S(1)}, s32[]{:S(2)}) async-start(s8[15728640]{0:T(1024)(128)(4,1)} %bitcast.190), calls=%async_computation.19 | async-start | bytes 8388608
  76.8 46.5 %slice-start.2 = ((s8[15728640]{0:T(1024)(128)(4,1)}), s8[4194304]{0:T(1024)(128)(4,1)S(1)}, s32[]{:S(2)}) async-start(s8[15728640]{0:T(1024)(128)(4,1)} %bitcast.190), calls=%async_computation.20 | async-start | bytes 8388608
  100.8 22.5 %copy-start.15 = (f32[2048]{0:T(1024)}, f32[2048]{0:T(1024)S(1)}, u32[]{:S(2)}) copy-start(f32[2048]{0:T(1024)S(1)} %get-tuple-element.37) | copy-start | bytes 24580
  100.8 161.2 %copy-start.13 = (f32[2048]{0:T(1024)}, f32[2048]{0:T(1024)S(1)}, u32[]{:S(2)}) copy-start(f32[2048]{0:T(1024)S(1)} %add_rsqrt_fusion) | copy-start | bytes 24580
  100.8 22.5 %slice-start.3 = ((s8[15728640]{0:T(1024)(128)(4,1)}), s8[4194304]{0:T(1024)(128)(4,1)S(1)}, s32[]{:S(2)}) async-start(s8[15728640]{0:T(1024)(128)(4,1)} %bitcast.190), calls=%async_computation.21 | async-start | bytes 8388608
  209.1 230.8 %reduce-scatter.7.cloned.1.call-start = ((), (), s32[]{:S(2)}) async-start(), calls=%async_computation.6 | async-start | bytes 8355840 | tf_op jit(solution)/shard_map/reduce_scatter | solution.py:41
  209.1 30.7 %slice-start.4 = ((s8[15728640]{0:T(1024)(128)(4,1)}), s8[3145728]{0:T(1024)(128)(4,1)S(1)}, s32[]{:S(2)}) async-start(s8[15728640]{0:T(1024)(128)(4,1)} %bitcast.192), calls=%async_computation.22 | async-start | bytes 6291456
  217.2 22.6 %slice-start.5 = ((s8[15728640]{0:T(1024)(128)(4,1)}), s8[4194304]{0:T(1024)(128)(4,1)S(1)}, s32[]{:S(2)}) async-start(s8[15728640]{0:T(1024)(128)(4,1)} %bitcast.192), calls=%async_computation.23 | async-start | bytes 8388608
  217.2 22.6 %slice-start.6 = ((s8[15728640]{0:T(1024)(128)(4,1)}), s8[4194304]{0:T(1024)(128)(4,1)S(1)}, s32[]{:S(2)}) async-start(s8[15728640]{0:T(1024)(128)(4,1)} %bitcast.192), calls=%async_computation.24 | async-start | bytes 8388608
  217.2 22.6 %slice-start.7 = ((s8[15728640]{0:T(1024)(128)(4,1)}), s8[4194304]{0:T(1024)(128)(4,1)S(1)}, s32[]{:S(2)}) async-start(s8[15728640]{0:T(1024)(128)(4,1)} %bitcast.192), calls=%async_computation.25 | async-start | bytes 8388608
  328.2 25.1 %copy-start.14 = (f32[2048]{0:T(1024)S(1)}, f32[2048]{0:T(1024)}, u32[]{:S(2)}) copy-start(f32[2048]{0:T(1024)} %copy-done.13) | copy-start | bytes 24580
  328.3 153.4 %reduce-scatter.11.cloned.1.call-start = ((), (), s32[]{:S(2)}) async-start(), calls=%async_computation.8 | async-start | bytes 8355840 | tf_op jit(solution)/shard_map/reduce_scatter | solution.py:41
  353.3 206.1 %reduce-scatter.13.cloned.1.call-start = ((), (), s32[]{:S(2)}) async-start(), calls=%async_computation.9 | async-start | bytes 8355840 | tf_op jit(solution)/shard_map/reduce_scatter | solution.py:41
  375.7 261.6 %reduce-scatter.15.cloned.1.call-start = ((), (), s32[]{:S(2)}) async-start(), calls=%async_computation.10 | async-start | bytes 8355840 | tf_op jit(solution)/shard_map/reduce_scatter | solution.py:41
  398.2 317.0 %reduce-scatter.17.cloned.1.call-start = ((), (), s32[]{:S(2)}) async-start(), calls=%async_computation.11 | async-start | bytes 8355840 | tf_op jit(solution)/shard_map/reduce_scatter | solution.py:41
  427.0 376.1 %all-gather.15.cloned.1.call-start = ((), (), s32[]{:S(2)}) async-start(), calls=%async_computation.16 | async-start | bytes 8355840 | tf_op jit(solution)/shard_map/all_gather | solution.py:73
  755.1 97.1 %all-gather.17.cloned.1.call-start = ((), (), s32[]{:S(2)}) async-start(), calls=%async_computation.17 | async-start | bytes 8355840 | tf_op jit(solution)/shard_map/all_gather | solution.py:73
  755.9 145.5 %all-gather.11.cloned.1.call-start = ((), (), s32[]{:S(2)}) async-start(), calls=%async_computation.14 | async-start | bytes 8355840 | tf_op jit(solution)/shard_map/all_gather | solution.py:73
  765.8 184.6 %all-gather.13.cloned.1.call-start = ((), (), s32[]{:S(2)}) async-start(), calls=%async_computation.15 | async-start | bytes 8355840 | tf_op jit(solution)/shard_map/all_gather | solution.py:73
  766.4 233.1 %all-gather.7.cloned.1.call-start = ((), (), s32[]{:S(2)}) async-start(), calls=%async_computation.12 | async-start | bytes 8355840 | tf_op jit(solution)/shard_map/all_gather | solution.py:73
  776.6 271.9 %all-gather.9.cloned.1.call-start = ((), (), s32[]{:S(2)}) async-start(), calls=%async_computation.13 | async-start | bytes 8355840 | tf_op jit(solution)/shard_map/all_gather | solution.py:73
  (15 other events, 156.4 us)
Sparse Core Ops, SparseCore 0:
  209.2 75.7 reduce-scatter.8
  328.4 75.7 reduce-scatter.6
  408.6 72.9 reduce-scatter.10
  486.5 72.9 reduce-scatter.12
  564.3 72.9 reduce-scatter.14
  642.1 72.9 reduce-scatter.16
  755.2 47.7 all-gather.14
  805.2 46.8 all-gather.16
  854.4 46.8 all-gather.10
  903.4 46.8 all-gather.12
  952.6 46.8 all-gather.6
  1001.6 46.8 all-gather.8

commit v2 on v1

v2 whole, which is shorter than its diff:
```python
import functools

import jax
import jax.numpy as jnp
from jax import lax
from jax.experimental import pallas as pl
from jax.experimental.pallas import tpu as pltpu
from jax.sharding import PartitionSpec as P

F32, BF16 = jnp.float32, jnp.bfloat16
MESH = pl.DeviceIdType.MESH
BITS = (8, 4, 2)
VMEM_BYTES = 60 * 1024 * 1024
IN_VMEM, IN_HBM = pl.BlockSpec(memory_space=pltpu.VMEM), pl.BlockSpec(memory_space=pl.ANY)


def flip(place, bit):
    return place + bit * (1 - 2 * lax.rem(lax.div(place, bit), 2))


def flips(place, axes, mask):
    for p, axis in enumerate(axes):
        if mask >> p & 1:
            place = flip(place, BITS[axis])
    return place


def meet(places):
    barrier = pltpu.get_barrier_semaphore()
    for place in places:
        pl.semaphore_signal(barrier, inc=1, device_id={"dp": place}, device_id_type=MESH)
    pl.semaphore_wait(barrier, len(places))


def remote(src, dst, send, recv, place):
    return pltpu.make_async_remote_copy(
        src_ref=src, dst_ref=dst, send_sem=send, recv_sem=recv, device_id={"dp": place}, device_id_type=MESH
    )


def turned(turn):
    return tuple((turn + p) % 3 for p in range(3))


def sum_into(dst, terms, rows):
    def body(i, _):
        at = pl.ds(pl.multiple_of(i * 16, 16), 16)
        total = terms[0][at, :].astype(F32)
        for term in terms[1:]:
            total = total + term[at, :].astype(F32)
        dst[at, :] = total.astype(BF16)
        return 0

    lax.fori_loop(0, rows // 16, body, 0)


def scatter_kernel(jobs, *refs):
    grads, outs, rest = refs[:jobs], refs[jobs : 2 * jobs], refs[2 * jobs :]
    own, paired, first, second, third = (rest[k * jobs : (k + 1) * jobs] for k in range(5))
    local_sem, send_pair, recv_pair, send, recv = rest[5 * jobs :]
    me = lax.axis_index("dp")
    core = lax.rem(me, 2)
    partner = flip(me, 1)
    near = [flip(me, bit) for bit in BITS]
    meet([*near, partner])

    order = (1, 3, 5, 7, 2, 6, 4, 0)
    loads, pairs, hops = {}, {}, {}
    for mask in order:
        for j in range(jobs):
            chip = lax.div(flips(me, turned(j), mask), 2)
            pairs[j, mask] = remote(
                grads[j].at[chip, 1 - core], paired[j].at[mask], send_pair.at[j, mask], recv_pair.at[j, mask], partner
            )
            pairs[j, mask].start()
            loads[j, mask] = pltpu.make_async_copy(grads[j].at[chip, core], own[j].at[mask], local_sem.at[j, mask])
            loads[j, mask].start()

    def hop(j, mask, stage):
        dst = (first, second, third)[stage][j].at[mask >> (stage + 1)]
        hops[j, mask] = remote(own[j].at[mask], dst, send.at[j, mask], recv.at[j, mask], near[turned(j)[stage]])
        hops[j, mask].start()

    def add(j, mask, stage):
        loads[j, mask].wait()
        pairs[j, mask].wait_recv()
        terms = [own[j].at[mask], paired[j].at[mask]]
        for s in range(stage):
            hops[j, mask + (1 << s)].wait_recv()
            terms.append((first, second, third)[s][j].at[mask >> (s + 1)])
        sum_into(outs[j] if mask == 0 else own[j].at[mask], terms, own[j].shape[1])

    for stage, masks in enumerate(((1, 3, 5, 7), (2, 6), (4,))):
        for mask in masks:
            for j in range(jobs):
                add(j, mask, stage)
                hop(j, mask, stage)
    for j in range(jobs):
        add(j, 0, 3)
    for copy in (*pairs.values(), *hops.values()):
        copy.wait_send()


def scatter(grads, collective_id):
    jobs = len(grads)
    shapes = [(g.shape[0] // 16, g.shape[1]) for g in grads]
    buffers = lambda n: [pltpu.VMEM((n, *shape), BF16) for shape in shapes]
    sems = pltpu.SemaphoreType.DMA((jobs, 8))
    sent = sum(r * c for r, c in shapes) * 2 * 15
    return pl.pallas_call(
        functools.partial(scatter_kernel, jobs),
        out_shape=[jax.ShapeDtypeStruct(shape, BF16) for shape in shapes],
        in_specs=[IN_HBM] * jobs,
        out_specs=[IN_VMEM] * jobs,
        scratch_shapes=[*buffers(8), *buffers(8), *buffers(4), *buffers(2), *buffers(1), *[sems] * 5],
        compiler_params=pltpu.CompilerParams(collective_id=collective_id, has_side_effects=True, vmem_limit_bytes=VMEM_BYTES),
        cost_estimate=pl.CostEstimate(flops=10**10, bytes_accessed=sent, transcendentals=0),
        name=f"scatter_{collective_id}",
    )(*[g.reshape(8, 2, *shape) for g, shape in zip(grads, shapes)])


def total_kernel(part_ref, out_ref, held, send, recv):
    me = lax.axis_index("dp")
    others = []
    for k in range(1, 16):
        place = me
        for bit in (1, 2, 4, 8):
            if k & bit:
                place = flip(place, bit)
        others.append(place)
    meet(others)
    copies = []
    for k, place in enumerate(others):
        copies.append(remote(part_ref, held.at[k + 1], send.at[k], recv.at[k], place))
        copies[-1].start()
    for copy in copies:
        copy.wait_recv()
    slots = [part_ref[...]] + [held[k] for k in range(1, 16)]
    while len(slots) > 1:
        slots = [slots[i] + slots[i + 1] for i in range(0, len(slots), 2)]
    out_ref[...] = slots[0]
    for copy in copies:
        copy.wait_send()


def total_of(part, collective_id):
    return pl.pallas_call(
        total_kernel,
        out_shape=jax.ShapeDtypeStruct((8, 128), F32),
        in_specs=[IN_VMEM],
        out_specs=IN_VMEM,
        scratch_shapes=[pltpu.VMEM((16, 8, 128), F32), pltpu.SemaphoreType.DMA((15,)), pltpu.SemaphoreType.DMA((15,))],
        compiler_params=pltpu.CompilerParams(collective_id=collective_id, has_side_effects=True),
        name="total",
    )(jnp.full((8, 128), part, F32))[0, 0]


def gather_kernel(count, layers, *refs):
    blocks, outs, rest = refs[:count], refs[count : 2 * count], refs[2 * count :]
    held, (local_sem, send, recv, send_pair, recv_pair) = rest[:count], rest[count:]
    me = lax.axis_index("dp")
    partner = flip(me, 1)
    near = [flip(me, bit) for bit in BITS]
    meet([*near, partner])
    jobs = [(i, l) for l in range(layers) for i in range(count)]

    def slot(i, l, mask):
        return held[i].at[l, mask - 1] if mask else blocks[i].at[l]

    def place_in(i, l, owner):
        rows = blocks[i].shape[1]
        return outs[i].at[l, pl.ds(pl.multiple_of(owner * rows, rows), rows), :]

    hops, pairs, locals_ = {}, {}, {}

    def hop(i, l, mask, stage):
        number = mask + (1 << stage)
        at = (l * count + i, number - 1)
        hops[i, l, number] = remote(slot(i, l, mask), slot(i, l, number), send.at[at], recv.at[at], near[turned(i)[stage]])
        hops[i, l, number].start()

    def hand_on(i, l, mask):
        owner = flips(me, turned(i), mask)
        at = (l * count + i, mask)
        pairs[i, l, mask] = remote(slot(i, l, mask), place_in(i, l, owner), send_pair.at[at], recv_pair.at[at], partner)
        pairs[i, l, mask].start()
        locals_[i, l, mask] = pltpu.make_async_copy(slot(i, l, mask), place_in(i, l, owner), local_sem.at[at])
        locals_[i, l, mask].start()

    for stage in range(3):
        for i, l in jobs:
            hop(i, l, 0, stage)
    for i, l in jobs:
        hand_on(i, l, 0)
    for mask in range(1, 8):
        for i, l in jobs:
            hops[i, l, mask].wait_recv()
            for stage in range(3):
                if mask < 1 << stage:
                    hop(i, l, mask, stage)
            hand_on(i, l, mask)
    for copy in pairs.values():
        copy.wait()
    for copy in hops.values():
        copy.wait_send()
    for copy in locals_.values():
        copy.wait()


def gather(blocks, collective_id):
    count, layers = len(blocks), blocks[0].shape[0]
    shapes = [b.shape[1:] for b in blocks]
    jobs = count * layers
    sent = sum(b.size for b in blocks) * 2 * 15
    return pl.pallas_call(
        functools.partial(gather_kernel, count, layers),
        out_shape=[jax.ShapeDtypeStruct((layers, 16 * r, c), BF16) for r, c in shapes],
        in_specs=[IN_VMEM] * count,
        out_specs=[IN_HBM] * count,
        scratch_shapes=[
            *[pltpu.VMEM((layers, 7, r, c), BF16) for r, c in shapes],
            pltpu.SemaphoreType.DMA((jobs, 8)),
            *[pltpu.SemaphoreType.DMA((jobs, 7))] * 2,
            *[pltpu.SemaphoreType.DMA((jobs, 8))] * 2,
        ],
        compiler_params=pltpu.CompilerParams(collective_id=collective_id, has_side_effects=True, vmem_limit_bytes=VMEM_BYTES),
        cost_estimate=pl.CostEstimate(flops=10**10, bytes_accessed=sent, transcendentals=0),
        name="gather",
    )(*blocks)


def dot(a, b, contract):
    return lax.dot_general(a, b, ((contract[:1], contract[1:]), ((), ())), preferred_element_type=F32)


def normed(h):
    wide = h.astype(F32)
    scale = lax.rsqrt(jnp.mean(wide**2, -1, keepdims=True) + 1e-6)
    return (wide * scale).astype(BF16), wide, scale


def gated(gate, up):
    return (jax.nn.silu(gate) * up).astype(BF16)


def gated_back(gate, up, d):
    d = d.astype(F32)
    s = jax.nn.sigmoid(gate)
    return (d * up * (s * (1 + gate * (1 - s)))).astype(BF16), (d * (gate * s)).astype(BF16)


def adamw(w, m, v, g):
    m = 0.9 * m + 0.1 * g
    v = 0.95 * v + 0.05 * g * g
    step = m * lax.rsqrt(v + 1e-8) + 0.1 * w
    return (w - 0.02 * step).astype(BF16), m, v


def solution(mesh):
    n = mesh.shape["dp"]

    def step(x, dy, wg, wu, wd, *moments):
        x, dy = x[0], dy[0]
        spread = lambda g: lax.psum_scatter(g.astype(BF16), "dp", scatter_dimension=0, tiled=True)
        a0, _, _ = normed(x)
        gate0, up0 = dot(a0, wg[0], (1, 0)), dot(a0, wu[0], (1, 0))
        hid0 = gated(gate0, up0)
        h1 = x + dot(hid0, wd[0], (1, 0)).astype(BF16)
        a1, wide1, scale1 = normed(h1)
        gate1, up1 = dot(a1, wg[1], (1, 0)), dot(a1, wu[1], (1, 0))
        hid1 = gated(gate1, up1)
        gd1 = spread(dot(hid1, dy, (0, 0)))
        dgate1, dup1 = gated_back(gate1, up1, dot(dy, wd[1], (1, 1)).astype(BF16))
        gg1 = spread(dot(a1, dgate1, (0, 0)))
        gu1 = spread(dot(a1, dup1, (0, 0)))
        da = dot(dgate1, wg[1], (1, 1)).astype(BF16) + dot(dup1, wu[1], (1, 1)).astype(BF16)
        da = da.astype(F32)
        dwide = scale1 * da - wide1 * (scale1**3 * jnp.mean(da * wide1, -1, keepdims=True))
        dh = dy + dwide.astype(BF16)
        gd0 = dot(hid0, dh, (0, 0)).astype(BF16)
        dgate0, dup0 = gated_back(gate0, up0, dot(dh, wd[0], (1, 1)).astype(BF16))
        gg0 = dot(a0, dgate0, (0, 0)).astype(BF16)
        gu0 = dot(a0, dup0, (0, 0)).astype(BF16)
        gg0, gu0, gd0 = scatter((gg0, gu0, gd0), 0)
        grads = [[g.astype(F32) for g in pair] for pair in ((gg0, gg1), (gu0, gu1), (gd0, gd1))]
        total = total_of(sum(jnp.sum(g * g) for pair in grads for g in pair), 1)
        count = wg.size + wu.size + wd.size
        factor = jnp.minimum(1.0, 0.5 * lax.rsqrt(total / count + 1e-30))
        me = lax.axis_index("dp")
        new_w, new_m, new_v = [], [], []
        for w, m, v, pair in zip((wg, wu, wd), moments[:3], moments[3:], grads):
            rows = w.shape[1] // n
            mine = lax.dynamic_slice_in_dim(w, me * rows, rows, 1)
            g = jnp.stack(pair) * factor
            for to, value in zip((new_w, new_m, new_v), adamw(mine.astype(F32), m, v, g)):
                to.append(value)
        new_w = gather(new_w, 2)
        return (*new_w, *new_m, *new_v)

    whole, rows = P(None, None, None), P(None, "dp", None)
    outs = (P("rep", None, None),) * 3 + (P("rep", "dp", None),) * 6
    return jax.shard_map(
        step, mesh=mesh, in_specs=(P(("rep", "dp"), None, None),) * 2 + (whole,) * 3 + (rows,) * 6, out_specs=outs, check_vma=False
    )
```

time: 1080 us -> 768 us (0.71)
  waiting for transfers between devices: 501 us -> 0.11 us
  Pallas kernels: 0 us -> 254 us
  other arithmetic: 87.7 us -> 43.1 us
  blocking collectives: 31.8 us -> 0 us
    reduce_scatter x6 -> x3, waiting for transfers between devices: 264 us -> 0.06 us  [step(): lax.psum_scatter(g.astype(BF16), 'dp', scatter_dimension=0, tiled=True)]
    pallas_call x0 -> x3, Pallas kernels: none -> 254 us  [the longest x1 157 us: gather(): pl.pallas_call(functools.partial(gather_kernel, count, layers), out_shape...]
    all_gather x6 -> x0, waiting for transfers between devices: 235 us -> none  [step(): full.append(lax.all_gather(nw, 'dp', axis=0, tiled=True))]
    another operation x6, other arithmetic: 49.9 us -> 4.53 us  [step(): g = jnp.stack(pair) * factor]
    psum x1 -> x0, blocking collectives: 31.8 us -> none  [step(): lax.psum(sum((jnp.sum(g * g) for pair in grads for g in pair)), 'dp')]
    unnamed x56 -> x37, local copies, waits for them, and re-layouts: 16.2 us -> 48 us
    slice x3 -> x1, local copies, waits for them, and re-layouts: 25.2 us -> 1.33 us  [total_of(): pl.pallas_call(total_kernel, out_shape=jax.ShapeDtypeStruct((8, 128), F32...]
  transfers between devices with their start and end apart: 12 -> 3, of which waited for: 10 -> 0; matrix products, arithmetic and copies ran while one was open for 28% -> 31% of each run, Pallas kernels for 0% -> 12%
where the time goes in v2:
time: 768 us; the launch traced here: 758 us
  matrix products  391 us (51%)
  Pallas kernels  254 us (33%)
  local copies, waits for them, and re-layouts  49.9 us (6%)
  other arithmetic  43.1 us (6%)
  between operations  19.7 us (3%)
    dot_general x15, matrix products, dot(): lax.dot_general(a, b, ((contract[:1], contract[1:]), ((), ())), preferred...  391 us
    pallas_call x1, Pallas kernels, gather(): pl.pallas_call(functools.partial(gather_kernel, count, layers), out_shape...  157 us
    pallas_call x1, Pallas kernels, scatter(): pl.pallas_call(functools.partial(scatter_kernel, jobs), out_shape=[jax.Sh...  90.1 us
    unnamed x37, local copies, waits for them, and re-layouts  48 us
  transfers between devices with their start and end apart: 3, of which 0 were waited for; matrix products, arithmetic and copies ran while one was open for 31% of the time, Pallas kernels for 12%

profile of v2, /device:TPU:0, one launch (start us, length us, event | category | flops | bytes accessed | tf_op | source)
XLA Modules:
  0.0 758.2 jit_solution(8567202073246962273)
XLA Ops:
  7.2 7.9 %copy.20 = bf16[1,2048,1280]{1,2,0:T(8,128)(2,1)} copy(bf16[1,2048,1280]{2,1,0:T(8,128)(2,1)} %param.11) | data formatting | bytes 10485760 | tf_op args[0]
  18.7 23.1 %fusion.41 = f32[2048,3072]{1,0:T(8,128)} fusion(bf16[2,1280,3072]{2,1,0:T(8,128)(2,1)} %param.13, bf16[1,2048,1280]{2,1,0:T(8,128)(2,1)} %param.11, f32[2048]{0:T(1024)S(1)} %add_rsqrt_fusion.1), kind=kOutput, calls=%fused_computation.56 | convolution fusion | flops 16113991680 | bytes 38281216 | tf_op jit(solution)/shard_map/dot_general | solution.py:233
  41.9 34.7 %multiply_convert_fusion.1 = (bf16[2048,3072]{1,0:T(8,128)(2,1)}, f32[2048,3072]{1,0:T(8,128)}) fusion(f32[2048,3072]{1,0:T(8,128)} %fusion.41, bf16[2,1280,3072]{2,1,0:T(8,128)(2,1)} %param.14, bf16[1,2048,1280]{2,1,0:T(8,128)(2,1)} %param.11, f32[2048]{0:T(1024)S(1)} %add_rsqrt_fusion.1), kind=kOutput, calls=%fused_computation.13 | convolution fusion | flops 16151740416 | bytes 76029952 | tf_op jit(solution)/shard_map/dot_general | solution.py:233
  76.6 22.7 %fusion.24 = (f32[2048]{0:T(1024)S(1)}, bf16[2048,1280]{0,1:T(8,128)(2,1)S(1)}) fusion(bf16[2048,3072]{1,0:T(8,128)(2,1)} %get-tuple-element.32, bf16[2,3072,1280]{2,1,0:T(8,128)(2,1)} %param.15, bf16[1,2048,1280]{1,2,0:T(8,128)(2,1)} %copy.20), kind=kOutput, calls=%fused_computation.38 | convolution fusion | flops 16119232512 | bytes 30941184 | tf_op jit(solution)/shard_map/dot_general | solution.py:233
  99.4 24.2 %convolution_convert_fusion.4 = bf16[2048,3072]{1,0:T(8,128)(2,1)} fusion(bf16[2,3072,1280]{2,1,0:T(8,128)(2,1)} %param.15, bf16[1,2048,1280]{2,1,0:T(8,128)(2,1)} %param.12), kind=kOutput, calls=%fused_computation.32 | convolution fusion | flops 16112418816 | bytes 25690112 | tf_op jit(solution)/shard_map/dot_general | solution.py:233
  123.5 22.2 %fusion.29 = f32[2048,3072]{1,0:T(8,128)} fusion(bf16[2,1280,3072]{2,1,0:T(8,128)(2,1)} %param.13, bf16[2048,1280]{0,1:T(8,128)(2,1)S(1)} %get-tuple-element.35, f32[2048]{0:T(1024)S(1)} %add_rsqrt_fusion), kind=kOutput, calls=%fused_computation.44 | convolution fusion | flops 16113991680 | bytes 38281216 | tf_op jit(solution)/shard_map/dot_general | solution.py:233
  145.7 42.7 %fusion.1 = (bf16[2048,3072]{1,0:T(8,128)(2,1)}, bf16[2048,3072]{1,0:T(8,128)(2,1)}, f32[2048,3072]{1,0:T(8,128)}) fusion(bf16[2048,3072]{1,0:T(8,128)(2,1)} %convolution_convert_fusion.4, f32[2048,3072]{1,0:T(8,128)} %fusion.29, bf16[2,1280,3072]{2,1,0:T(8,128)(2,1)} %param.14, bf16[2048,1280]{0,1:T(8,128)(2,1)} %copy-done.1, f32[2048]{0:T(1024)S(1)} %add_rsqrt_fusion), kind=kOutput, calls=%fused_computation.5 | convolution fusion | flops 16202072064 | bytes 101195776 | tf_op jit(solution)/shard_map/dot_general | solution.py:233
  188.4 22.3 %convolution_convert_fusion.2 = bf16[1280,3072]{1,0:T(8,128)(2,1)} fusion(bf16[2048,3072]{1,0:T(8,128)(2,1)} %get-tuple-element.30, bf16[2048,1280]{0,1:T(8,128)(2,1)} %copy-done.1, f32[2048]{0:T(1024)S(1)} %add_rsqrt_fusion), kind=kOutput, calls=%fused_computation.30 | convolution fusion | flops 16117923840 | bytes 25698304 | tf_op jit(solution)/shard_map/dot_general | solution.py:233
  210.8 22.2 %convolution_convert_fusion.1 = bf16[1280,3072]{1,0:T(8,128)(2,1)} fusion(bf16[2048,3072]{1,0:T(8,128)(2,1)} %get-tuple-element.31, bf16[2048,1280]{0,1:T(8,128)(2,1)} %copy-done.1, f32[2048]{0:T(1024)S(1)} %add_rsqrt_fusion), kind=kOutput, calls=%fused_computation.29 | convolution fusion | flops 16117923840 | bytes 25698304 | tf_op jit(solution)/shard_map/dot_general | solution.py:233
  233.0 28.6 %fusion.16 = bf16[3072,1280]{1,0:T(8,128)(2,1)} fusion(f32[2048,3072]{1,0:T(8,128)} %get-tuple-element.36, bf16[1,2048,1280]{2,1,0:T(8,128)(2,1)} %param.12, f32[2048,3072]{1,0:T(8,128)} %fusion.29), kind=kOutput, calls=%fused_computation.28 | convolution fusion | flops 16147808256 | bytes 63438848 | tf_op jit(solution)/shard_map/dot_general | solution.py:233
  261.7 22.5 %fusion.49 = bf16[2048,1280]{0,1:T(8,128)(2,1)} fusion(bf16[2048,3072]{1,0:T(8,128)(2,1)} %get-tuple-element.31, bf16[2,1280,3072]{2,1,0:T(8,128)(2,1)} %param.14), kind=kOutput, calls=%fused_computation.62 | convolution fusion | flops 16108748800 | bytes 25690112 | tf_op jit(solution)/shard_map/dot_general | solution.py:233
  284.2 7.9 %copy.21 = bf16[1,2048,1280]{1,2,0:T(8,128)(2,1)} copy(bf16[1,2048,1280]{2,1,0:T(8,128)(2,1)} %param.12) | data formatting | bytes 10485760 | tf_op args[1]
  292.1 24.9 %fusion.26 = (f32[2048]{0:T(1024)S(1)}, bf16[2048,1280]{0,1:T(8,128)(2,1)}) fusion(bf16[2048,1280]{0,1:T(8,128)(2,1)} %copy-done.1, bf16[2048,1280]{0,1:T(8,128)(2,1)} %fusion.49, bf16[2048,3072]{1,0:T(8,128)(2,1)} %get-tuple-element.30, bf16[2,1280,3072]{2,1,0:T(8,128)(2,1)} %param.13), kind=kOutput, calls=%fused_computation.40 | convolution fusion | flops 16121853952 | bytes 36184064 | tf_op jit(solution)/shard_map/dot_general | solution.py:233
  317.0 12.3 %fusion.68 = bf16[2048,1280]{0,1:T(8,128)(2,1)} fusion(bf16[2048,1280]{0,1:T(8,128)(2,1)} %copy-done.1, bf16[2048,1280]{0,1:T(8,128)(2,1)} %get-tuple-element.38, bf16[1,2048,1280]{1,2,0:T(8,128)(2,1)} %copy.21, f32[2048]{0:T(1024)S(1)} %fusion.99, f32[2048]{0:T(1024)S(1)} %add_rsqrt_fusion), kind=kLoop, calls=%fused_computation.73 | loop fusion | flops 18350080 | bytes 20987904 | tf_op jit(solution)/shard_map/add | solution.py:279
  329.4 22.6 %convolution_convert_fusion.3 = bf16[2048,3072]{1,0:T(8,128)(2,1)} fusion(bf16[2048,1280]{0,1:T(8,128)(2,1)} %fusion.68, bf16[2,3072,1280]{2,1,0:T(8,128)(2,1)} %param.15), kind=kOutput, calls=%fused_computation.31 | convolution fusion | flops 16112418816 | bytes 25690112 | tf_op jit(solution)/shard_map/dot_general | solution.py:233
  351.9 30.7 %fusion.17 = bf16[1280,3072]{1,0:T(8,128)(2,1)} fusion(f32[2048,3072]{1,0:T(8,128)} %get-tuple-element.33, bf16[2048,3072]{1,0:T(8,128)(2,1)} %convolution_convert_fusion.3, f32[2048,3072]{1,0:T(8,128)} %fusion.41, bf16[1,2048,1280]{1,2,0:T(8,128)(2,1)} %copy.20, f32[2048]{0:T(1024)S(1)} %copy-done.11), kind=kOutput, calls=%fused_computation.33 | convolution fusion | flops 16187129856 | bytes 76029952 | tf_op jit(solution)/shard_map/dot_general | solution.py:233
  382.6 22.5 %convolution_convert_fusion = bf16[3072,1280]{1,0:T(8,128)(2,1)} fusion(bf16[2048,3072]{1,0:T(8,128)(2,1)} %get-tuple-element.32, bf16[2048,1280]{0,1:T(8,128)(2,1)} %fusion.68), kind=kOutput, calls=%fused_computation.26 | convolution fusion | flops 16110059520 | bytes 25690112 | tf_op jit(solution)/shard_map/dot_general | solution.py:233
  405.2 24.9 %fusion.13 = bf16[1280,3072]{1,0:T(8,128)(2,1)} fusion(bf16[2048,3072]{1,0:T(8,128)(2,1)} %convolution_convert_fusion.3, bf16[1,2048,1280]{1,2,0:T(8,128)(2,1)} %copy.20, f32[2048]{0:T(1024)S(1)} %copy-done.11, f32[2048,3072]{1,0:T(8,128)} %fusion.41), kind=kOutput, calls=%fused_computation.27 | convolution fusion | flops 16161964032 | bytes 50864128 | tf_op jit(solution)/shard_map/dot_general | solution.py:233
  430.1 90.1 %scatter_0.1 = (bf16[80,3072]{1,0:T(8,128)(2,1)}, bf16[80,3072]{1,0:T(8,128)(2,1)}, bf16[192,1280]{1,0:T(8,128)(2,1)}) custom-call(bf16[8,2,80,3072]{3,2,1,0:T(8,128)(2,1)} %bitcast.88, bf16[8,2,80,3072]{3,2,1,0:T(8,128)(2,1)} %bitcast.90, bf16[8,2,192,1280]{3,2,1,0:T(8,128)(2,1)} %bitcast.89), custom_call_target="tpu_custom_call" | custom-call | flops 10000000000 | bytes 22118400 | tf_op jit(solution)/shard_map/scatter_0/pallas_call | solution.py:110
  539.5 7.3 total.1
  556.0 6.0 fusion.83
  562.0 157.1 %gather.1 = (bf16[2,1280,3072]{2,1,0:T(8,128)(2,1)}, bf16[2,1280,3072]{2,1,0:T(8,128)(2,1)}, bf16[2,3072,1280]{2,1,0:T(8,128)(2,1)}) custom-call(bf16[2,80,3072]{2,1,0:T(8,128)(2,1)} %get-tuple-element.27.refs_0_, bf16[2,80,3072]{2,1,0:T(8,128)(2,1)} %get-tuple-element.39.refs_1_, bf16[2,192,1280]{2,1,0:T(8,128)(2,1)} %get-tuple-element.21.refs_2_), custom_call_target="tpu_custom_call" | custom-call | flops 10000000000 | bytes 44236800 | tf_op jit(solution)/shard_map/gather/pallas_call | solution.py:215
  719.2 15.9 %copy.25 = bf16[2,1280,3072]{2,1,0:T(8,128)(2,1)} copy(bf16[2,1280,3072]{2,1,0:T(8,128)(2,1)} %get-tuple-element.51) | data formatting | bytes 31457280
  735.0 8.0 %copy.26 = bf16[2,1280,3072]{2,1,0:T(8,128)(2,1)} copy(bf16[2,1280,3072]{2,1,0:T(8,128)(2,1)S(1)} %copy-done) | data formatting | bytes 31457280
  (62 shorter events, 35.2 us)
Async XLA Ops:
  7.2 522.0 %reduce-scatter.4.cloned.1.call-start = ((), (), s32[]{:S(2)}) async-start(), calls=%async_computation.3 | async-start | bytes 8355840 | tf_op jit(solution)/shard_map/reduce_scatter | solution.py:264
  18.7 23.1 %copy-start.10 = (f32[2048]{0:T(1024)}, f32[2048]{0:T(1024)S(1)}, u32[]{:S(2)}) copy-start(f32[2048]{0:T(1024)S(1)} %add_rsqrt_fusion.1) | copy-start | bytes 24580
  99.3 24.2 %copy-start.8 = (f32[2048]{0:T(1024)}, f32[2048]{0:T(1024)S(1)}, u32[]{:S(2)}) copy-start(f32[2048]{0:T(1024)S(1)} %get-tuple-element.34) | copy-start | bytes 24580
  99.3 24.2 %copy-start.1 = (bf16[2048,1280]{0,1:T(8,128)(2,1)}, bf16[2048,1280]{0,1:T(8,128)(2,1)S(1)}, u32[]{:S(2)}) copy-start(bf16[2048,1280]{0,1:T(8,128)(2,1)S(1)} %get-tuple-element.35) | copy-start | bytes 15728644
  210.8 322.3 %reduce-scatter.6.cloned.1.call-start = ((), (), s32[]{:S(2)}) async-start(), calls=%async_computation.4 | async-start | bytes 8355840 | tf_op jit(solution)/shard_map/reduce_scatter | solution.py:264
  233.0 303.3 %reduce-scatter.8.cloned.1.call-start = ((), (), s32[]{:S(2)}) async-start(), calls=%async_computation.5 | async-start | bytes 8355840 | tf_op jit(solution)/shard_map/reduce_scatter | solution.py:264
  292.1 24.9 %copy-start.9 = (f32[2048]{0:T(1024)S(1)}, f32[2048]{0:T(1024)}, u32[]{:S(2)}) copy-start(f32[2048]{0:T(1024)} %copy-done.8) | copy-start | bytes 24580
  329.4 22.6 %copy-start.11 = (f32[2048]{0:T(1024)S(1)}, f32[2048]{0:T(1024)}, u32[]{:S(2)}) copy-start(f32[2048]{0:T(1024)} %copy-done.10) | copy-start | bytes 24580
  529.2 26.7 %copy-start.6 = (bf16[80,3072]{1,0:T(8,128)(2,1)S(1)}, bf16[80,3072]{1,0:T(8,128)(2,1)}, u32[]{:S(2)}) copy-start(bf16[80,3072]{1,0:T(8,128)(2,1)} %reduce-scatter.4.cloned.1.call-done) | copy-start | bytes 1474564
  546.7 9.1 %copy-start.7 = (bf16[80,3072]{1,0:T(8,128)(2,1)S(1)}, bf16[80,3072]{1,0:T(8,128)(2,1)}, u32[]{:S(2)}) copy-start(bf16[80,3072]{1,0:T(8,128)(2,1)} %reduce-scatter.6.cloned.1.call-done) | copy-start | bytes 1474564
  546.7 9.2 %copy-start.2 = (f32[2,80,3072]{2,1,0:T(8,128)S(1)}, f32[2,80,3072]{2,1,0:T(8,128)}, u32[]{:S(2)}) copy-start(f32[2,80,3072]{2,1,0:T(8,128)} %param.19) | copy-start | bytes 5898244
  546.7 9.2 %copy-start.3 = (f32[2,80,3072]{2,1,0:T(8,128)S(1)}, f32[2,80,3072]{2,1,0:T(8,128)}, u32[]{:S(2)}) copy-start(f32[2,80,3072]{2,1,0:T(8,128)} %param.16) | copy-start | bytes 5898244
  546.8 9.2 %copy-start.4 = (f32[2,80,3072]{2,1,0:T(8,128)S(1)}, f32[2,80,3072]{2,1,0:T(8,128)}, u32[]{:S(2)}) copy-start(f32[2,80,3072]{2,1,0:T(8,128)} %param.20) | copy-start | bytes 5898244
  546.8 9.2 %copy-start.5 = (f32[2,80,3072]{2,1,0:T(8,128)S(1)}, f32[2,80,3072]{2,1,0:T(8,128)}, u32[]{:S(2)}) copy-start(f32[2,80,3072]{2,1,0:T(8,128)} %param.17) | copy-start | bytes 5898244
  719.1 15.9 %copy-start = (bf16[2,1280,3072]{2,1,0:T(8,128)(2,1)S(1)}, bf16[2,1280,3072]{2,1,0:T(8,128)(2,1)}, u32[]{:S(2)}) copy-start(bf16[2,1280,3072]{2,1,0:T(8,128)(2,1)} %get-tuple-element.52) | copy-start | bytes 47185924
  719.1 23.9 %slice-start = ((s8[15728640]{0:T(1024)(128)(4,1)}), s8[4194304]{0:T(1024)(128)(4,1)S(1)}, s32[]{:S(2)}) async-start(s8[15728640]{0:T(1024)(128)(4,1)} %bitcast.86), calls=%async_computation.6 | async-start | bytes 8388608
  719.2 23.9 %slice-start.1 = ((s8[15728640]{0:T(1024)(128)(4,1)}), s8[4194304]{0:T(1024)(128)(4,1)S(1)}, s32[]{:S(2)}) async-start(s8[15728640]{0:T(1024)(128)(4,1)} %bitcast.86), calls=%async_computation.7 | async-start | bytes 8388608
  735.0 9.5 %slice-start.2 = ((s8[15728640]{0:T(1024)(128)(4,1)}), s8[4194304]{0:T(1024)(128)(4,1)S(1)}, s32[]{:S(2)}) async-start(s8[15728640]{0:T(1024)(128)(4,1)} %bitcast.86), calls=%async_computation.8 | async-start | bytes 8388608
  735.0 10.4 %slice-start.3 = ((s8[15728640]{0:T(1024)(128)(4,1)}), s8[3145728]{0:T(1024)(128)(4,1)S(1)}, s32[]{:S(2)}) async-start(s8[15728640]{0:T(1024)(128)(4,1)} %bitcast.86), calls=%async_computation.9 | async-start | bytes 6291456
Sparse Core Ops, SparseCore 0:
  210.9 75.8 reduce-scatter.3
  291.1 72.9 reduce-scatter.5
  368.6 76.2 reduce-scatter.7

commit v3 on v2

--- a/solution.py
+++ b/solution.py
@@ -54,31 +54,32 @@
     lax.fori_loop(0, rows // 16, body, 0)
 
 
-def scatter_kernel(jobs, *refs):
-    grads, outs, rest = refs[:jobs], refs[jobs : 2 * jobs], refs[2 * jobs :]
-    own, paired, first, second, third = (rest[k * jobs : (k + 1) * jobs] for k in range(5))
-    local_sem, send_pair, recv_pair, send, recv = rest[5 * jobs :]
+def scatter_kernel(count, jobs, *refs):
+    grads, outs, rest = refs[:count], refs[count : 2 * count], refs[2 * count :]
+    n = len(jobs)
+    own, paired, first, second, third = (rest[k * n : (k + 1) * n] for k in range(5))
+    local_sem, send_pair, recv_pair, send, recv = rest[5 * n :]
     me = lax.axis_index("dp")
     core = lax.rem(me, 2)
     partner = flip(me, 1)
     near = [flip(me, bit) for bit in BITS]
     meet([*near, partner])
 
-    order = (1, 3, 5, 7, 2, 6, 4, 0)
+    axes = [turned(turn) for _, _, _, turn in jobs]
     loads, pairs, hops = {}, {}, {}
-    for mask in order:
-        for j in range(jobs):
-            chip = lax.div(flips(me, turned(j), mask), 2)
+    for mask in (1, 3, 5, 7, 2, 6, 4, 0):
+        for j, (i, start, width, _) in enumerate(jobs):
+            chip, columns = lax.div(flips(me, axes[j], mask), 2), pl.ds(start, width)
             pairs[j, mask] = remote(
-                grads[j].at[chip, 1 - core], paired[j].at[mask], send_pair.at[j, mask], recv_pair.at[j, mask], partner
+                grads[i].at[chip, 1 - core, :, columns], paired[j].at[mask], send_pair.at[j, mask], recv_pair.at[j, mask], partner
             )
             pairs[j, mask].start()
-            loads[j, mask] = pltpu.make_async_copy(grads[j].at[chip, core], own[j].at[mask], local_sem.at[j, mask])
+            loads[j, mask] = pltpu.make_async_copy(grads[i].at[chip, core, :, columns], own[j].at[mask], local_sem.at[j, mask])
             loads[j, mask].start()
 
     def hop(j, mask, stage):
         dst = (first, second, third)[stage][j].at[mask >> (stage + 1)]
-        hops[j, mask] = remote(own[j].at[mask], dst, send.at[j, mask], recv.at[j, mask], near[turned(j)[stage]])
+        hops[j, mask] = remote(own[j].at[mask], dst, send.at[j, mask], recv.at[j, mask], near[axes[j][stage]])
         hops[j, mask].start()
 
     def add(j, mask, stage):
@@ -88,30 +89,31 @@
         for s in range(stage):
             hops[j, mask + (1 << s)].wait_recv()
             terms.append((first, second, third)[s][j].at[mask >> (s + 1)])
-        sum_into(outs[j] if mask == 0 else own[j].at[mask], terms, own[j].shape[1])
+        i, start, width, _ = jobs[j]
+        sum_into(outs[i].at[:, pl.ds(start, width)] if mask == 0 else own[j].at[mask], terms, own[j].shape[1])
 
     for stage, masks in enumerate(((1, 3, 5, 7), (2, 6), (4,))):
         for mask in masks:
-            for j in range(jobs):
+            for j in range(n):
                 add(j, mask, stage)
                 hop(j, mask, stage)
-    for j in range(jobs):
+    for j in range(n):
         add(j, 0, 3)
     for copy in (*pairs.values(), *hops.values()):
         copy.wait_send()
 
 
-def scatter(grads, collective_id):
-    jobs = len(grads)
+def scatter(grads, jobs, collective_id):
+    count = len(grads)
     shapes = [(g.shape[0] // 16, g.shape[1]) for g in grads]
-    buffers = lambda n: [pltpu.VMEM((n, *shape), BF16) for shape in shapes]
-    sems = pltpu.SemaphoreType.DMA((jobs, 8))
+    buffers = lambda n: [pltpu.VMEM((n, shapes[i][0], width), BF16) for i, _, width, _ in jobs]
+    sems = pltpu.SemaphoreType.DMA((len(jobs), 8))
     sent = sum(r * c for r, c in shapes) * 2 * 15
     return pl.pallas_call(
-        functools.partial(scatter_kernel, jobs),
+        functools.partial(scatter_kernel, count, jobs),
         out_shape=[jax.ShapeDtypeStruct(shape, BF16) for shape in shapes],
-        in_specs=[IN_HBM] * jobs,
-        out_specs=[IN_VMEM] * jobs,
+        in_specs=[IN_HBM] * count,
+        out_specs=[IN_VMEM] * count,
         scratch_shapes=[*buffers(8), *buffers(8), *buffers(4), *buffers(2), *buffers(1), *[sems] * 5],
         compiler_params=pltpu.CompilerParams(collective_id=collective_id, has_side_effects=True, vmem_limit_bytes=VMEM_BYTES),
         cost_estimate=pl.CostEstimate(flops=10**10, bytes_accessed=sent, transcendentals=0),
@@ -119,7 +121,8 @@
     )(*[g.reshape(8, 2, *shape) for g, shape in zip(grads, shapes)])
 
 
-def total_kernel(part_ref, out_ref, held, send, recv):
+def total_kernel(count, *refs):
+    grads, (out_ref, part_ref, held, send, recv) = refs[:count], refs[count:]
     me = lax.axis_index("dp")
     others = []
     for k in range(1, 16):
@@ -128,31 +131,48 @@
             if k & bit:
                 place = flip(place, bit)
         others.append(place)
+    sums = jnp.zeros((8, 128), F32)
+    for grad in grads:
+        rows, columns = grad.shape
+
+        def body(i, sums, grad=grad, columns=columns):
+            g = grad[pl.ds(pl.multiple_of(i * 16, 16), 16), :].astype(F32)
+            g = g * g
+            g = g[:8] + g[8:]
+            tiles = [g[:, c : c + 128] for c in range(0, columns, 128)]
+            while len(tiles) > 1:
+                tiles = [sum(tiles[c : c + 2]) for c in range(0, len(tiles), 2)]
+            return sums + tiles[0]
+
+        sums = lax.fori_loop(0, rows // 16, body, sums)
+    part_ref[...] = sums
     meet(others)
     copies = []
     for k, place in enumerate(others):
-        copies.append(remote(part_ref, held.at[k + 1], send.at[k], recv.at[k], place))
+        copies.append(remote(part_ref, held.at[k], send.at[k], recv.at[k], place))
         copies[-1].start()
     for copy in copies:
         copy.wait_recv()
-    slots = [part_ref[...]] + [held[k] for k in range(1, 16)]
+    slots = [part_ref[...]] + [held[k] for k in range(15)]
     while len(slots) > 1:
         slots = [slots[i] + slots[i + 1] for i in range(0, len(slots), 2)]
-    out_ref[...] = slots[0]
+    out_ref[...] = jnp.zeros((8, 128), F32) + jnp.sum(slots[0])
     for copy in copies:
         copy.wait_send()
 
 
-def total_of(part, collective_id):
+def total_of(grads, collective_id):
     return pl.pallas_call(
-        total_kernel,
+        functools.partial(total_kernel, len(grads)),
         out_shape=jax.ShapeDtypeStruct((8, 128), F32),
-        in_specs=[IN_VMEM],
+        in_specs=[IN_VMEM] * len(grads),
         out_specs=IN_VMEM,
-        scratch_shapes=[pltpu.VMEM((16, 8, 128), F32), pltpu.SemaphoreType.DMA((15,)), pltpu.SemaphoreType.DMA((15,))],
+        scratch_shapes=[
+            pltpu.VMEM((8, 128), F32), pltpu.VMEM((15, 8, 128), F32), pltpu.SemaphoreType.DMA((15,)), pltpu.SemaphoreType.DMA((15,))
+        ],
         compiler_params=pltpu.CompilerParams(collective_id=collective_id, has_side_effects=True),
         name="total",
-    )(jnp.full((8, 128), part, F32))[0, 0]
+    )(*grads)[0, 0]
 
 
 def gather_kernel(count, layers, *refs):
@@ -233,20 +253,158 @@
     return lax.dot_general(a, b, ((contract[:1], contract[1:]), ((), ())), preferred_element_type=F32)
 
 
+def scale_of(wide):
+    return lax.rsqrt(jnp.mean(wide * wide, -1, keepdims=True) + 1e-6)
+
+
 def normed(h):
     wide = h.astype(F32)
-    scale = lax.rsqrt(jnp.mean(wide**2, -1, keepdims=True) + 1e-6)
-    return (wide * scale).astype(BF16), wide, scale
-
-
-def gated(gate, up):
-    return (jax.nn.silu(gate) * up).astype(BF16)
+    return (wide * scale_of(wide)).astype(BF16)
 
 
 def gated_back(gate, up, d):
-    d = d.astype(F32)
     s = jax.nn.sigmoid(gate)
     return (d * up * (s * (1 + gate * (1 - s)))).astype(BF16), (d * (gate * s)).astype(BF16)
+
+
+def run(kernel, name, grid, ins, outs, flops):
+    moved = sum(a.size * a.dtype.itemsize for a, _, _ in ins)
+    return pl.pallas_call(
+        kernel,
+        grid=grid,
+        in_specs=[pl.BlockSpec(block, index) for _, block, index in ins],
+        out_specs=[pl.BlockSpec(block, index) for _, _, block, index in outs],
+        out_shape=[jax.ShapeDtypeStruct(shape, kind) for shape, kind, _, _ in outs],
+        compiler_params=pltpu.CompilerParams(dimension_semantics=("arbitrary",) * len(grid), vmem_limit_bytes=VMEM_BYTES),
+        cost_estimate=pl.CostEstimate(flops=flops, bytes_accessed=moved, transcendentals=0),
+        name=name,
+    )(*[a for a, _, _ in ins])
+
+
+def pieces(width, piece):
+    return [pl.ds(at, piece) for at in range(0, width, piece)]
+
+
+def up_kernel(x_ref, wg_ref, wu_ref, a_ref, gate_ref, up_ref, hid_ref):
+    @pl.when(pl.program_id(1) == 0)
+    def _():
+        def body(i, _):
+            at = pl.ds(pl.multiple_of(i * 128, 128), 128)
+            a_ref[at, :] = normed(x_ref[at, :])
+            return 0
+
+        lax.fori_loop(0, x_ref.shape[0] // 128, body, 0)
+
+    for at in pieces(gate_ref.shape[1], 256):
+        gate, up = dot(a_ref[...], wg_ref[0, :, at], (1, 0)), dot(a_ref[...], wu_ref[0, :, at], (1, 0))
+        gate_ref[:, at] = gate
+        up_ref[:, at] = up
+        hid_ref[:, at] = (gate * jax.nn.sigmoid(gate) * up).astype(BF16)
+
+
+def up_layer(x, wg, wu, l):
+    (t, d), f = x.shape, wg.shape[2]
+    tm, tn = 1024, 512
+    row, weight, tile = (lambda i, j: (i, 0)), (lambda i, j: (l, 0, j)), (lambda i, j: (i, j))
+    return run(
+        up_kernel, "up", (t // tm, f // tn),
+        [(x, (tm, d), row), (wg, (1, d, tn), weight), (wu, (1, d, tn), weight)],
+        [((t, d), BF16, (tm, d), row), *[((t, f), kind, (tm, tn), tile) for kind in (F32, F32, BF16)]],
+        4 * t * d * f,
+    )
+
+
+def down_kernel(hid_ref, w_ref, x_ref, h_ref, a_ref):
+    half = hid_ref.shape[0] // 2
+    for at in (pl.ds(0, half), pl.ds(half, half)):
+        h = x_ref[at, :] + dot(hid_ref[at, :], w_ref[0], (1, 0)).astype(BF16)
+        h_ref[at, :] = h
+        a_ref[at, :] = normed(h)
+
+
+def down_layer(hid, wd, x, l):
+    (t, f), d = hid.shape, wd.shape[2]
+    tm = 512
+    row = lambda i: (i, 0)
+    return run(
+        down_kernel, "down", (t // tm,),
+        [(hid, (tm, f), row), (wd, (1, f, d), lambda i: (l, 0, 0)), (x, (tm, d), row)],
+        [((t, d), BF16, (tm, d), row)] * 2,
+        2 * t * d * f,
+    )
+
+
+def turn_kernel(a_ref, dy_ref, wg_ref, wu_ref, wd_ref, hid_ref, dgate_ref, dup_ref):
+    for at in pieces(hid_ref.shape[1], 256):
+        gate, up = dot(a_ref[...], wg_ref[0, :, at], (1, 0)), dot(a_ref[...], wu_ref[0, :, at], (1, 0))
+        d = dot(dy_ref[...], wd_ref[0, at, :], (1, 1)).astype(BF16).astype(F32)
+        hid_ref[:, at] = (gate * jax.nn.sigmoid(gate) * up).astype(BF16)
+        dgate_ref[:, at], dup_ref[:, at] = gated_back(gate, up, d)
+
+
+def turn_layer(a, dy, wg, wu, wd, l):
+    (t, d), f = a.shape, wg.shape[2]
+    tm, tn = 1024, 512
+    row, weight, tile = (lambda i, j: (i, 0)), (lambda i, j: (l, 0, j)), (lambda i, j: (i, j))
+    return run(
+        turn_kernel, "turn", (t // tm, f // tn),
+        [(a, (tm, d), row), (dy, (tm, d), row), *[(w, (1, d, tn), weight) for w in (wg, wu)], (wd, (1, tn, d), lambda i, j: (l, j, 0))],
+        [((t, f), BF16, (tm, tn), tile)] * 3,
+        6 * t * d * f,
+    )
+
+
+def back_kernel(dgate_ref, dup_ref, wg_ref, wu_ref, h_ref, dy_ref, dh_ref):
+    da = dot(dgate_ref[...], wg_ref[0], (1, 1)).astype(BF16) + dot(dup_ref[...], wu_ref[0], (1, 1)).astype(BF16)
+    da, wide = da.astype(F32), h_ref[...].astype(F32)
+    scale = scale_of(wide)
+    dwide = scale * da - wide * (scale * scale * scale * jnp.mean(da * wide, -1, keepdims=True))
+    dh_ref[...] = dy_ref[...] + dwide.astype(BF16)
+
+
+def back_layer(dgate, dup, wg, wu, h, dy, l):
+    (t, f), d = dgate.shape, wg.shape[1]
+    tm = 512
+    row = lambda i: (i, 0)
+    return run(
+        back_kernel, "back", (t // tm,),
+        [*[(g, (tm, f), row) for g in (dgate, dup)], *[(w, (1, d, f), lambda i: (l, 0, 0)) for w in (wg, wu)], (h, (tm, d), row), (dy, (tm, d), row)],
+        [((t, d), BF16, (tm, d), row)],
+        4 * t * d * f,
+    )[0]
+
+
+def hidden_kernel(dh_ref, wd_ref, gate_ref, up_ref, dgate_ref, dup_ref):
+    for at in pieces(gate_ref.shape[1], 256):
+        d = dot(dh_ref[...], wd_ref[0, at, :], (1, 1)).astype(BF16).astype(F32)
+        dgate_ref[:, at], dup_ref[:, at] = gated_back(gate_ref[:, at], up_ref[:, at], d)
+
+
+def hidden_back(dh, wd, gate, up, l):
+    (t, d), f = dh.shape, gate.shape[1]
+    tm, tn = 1024, 512
+    row, tile = (lambda i, j: (i, 0)), (lambda i, j: (i, j))
+    return run(
+        hidden_kernel, "hidden", (t // tm, f // tn),
+        [(dh, (tm, d), row), (wd, (1, tn, d), lambda i, j: (l, j, 0)), (gate, (tm, tn), tile), (up, (tm, tn), tile)],
+        [((t, f), BF16, (tm, tn), tile)] * 2,
+        2 * t * d * f,
+    )
+
+
+def weight_kernel(a_ref, b_ref, out_ref):
+    out_ref[...] = dot(a_ref[...], b_ref[...], (0, 0)).astype(BF16)
+
+
+def weight_grad(a, b):
+    (t, p), q = a.shape, b.shape[1]
+    tp, tq = (640, 1024) if p < q else (768, 1280)
+    return run(
+        weight_kernel, "weight", (p // tp, q // tq),
+        [(a, (t, tp), lambda i, j: (0, i)), (b, (t, tq), lambda i, j: (0, j))],
+        [((p, q), BF16, (tp, tq), lambda i, j: (i, j))],
+        2 * t * p * q,
+    )[0]
 
 
 def adamw(w, m, v, g):
@@ -261,29 +419,22 @@
 
     def step(x, dy, wg, wu, wd, *moments):
         x, dy = x[0], dy[0]
-        spread = lambda g: lax.psum_scatter(g.astype(BF16), "dp", scatter_dimension=0, tiled=True)
-        a0, _, _ = normed(x)
-        gate0, up0 = dot(a0, wg[0], (1, 0)), dot(a0, wu[0], (1, 0))
-        hid0 = gated(gate0, up0)
-        h1 = x + dot(hid0, wd[0], (1, 0)).astype(BF16)
-        a1, wide1, scale1 = normed(h1)
-        gate1, up1 = dot(a1, wg[1], (1, 0)), dot(a1, wu[1], (1, 0))
-        hid1 = gated(gate1, up1)
-        gd1 = spread(dot(hid1, dy, (0, 0)))
-        dgate1, dup1 = gated_back(gate1, up1, dot(dy, wd[1], (1, 1)).astype(BF16))
-        gg1 = spread(dot(a1, dgate1, (0, 0)))
-        gu1 = spread(dot(a1, dup1, (0, 0)))
-        da = dot(dgate1, wg[1], (1, 1)).astype(BF16) + dot(dup1, wu[1], (1, 1)).astype(BF16)
-        da = da.astype(F32)
-        dwide = scale1 * da - wide1 * (scale1**3 * jnp.mean(da * wide1, -1, keepdims=True))
-        dh = dy + dwide.astype(BF16)
-        gd0 = dot(hid0, dh, (0, 0)).astype(BF16)
-        dgate0, dup0 = gated_back(gate0, up0, dot(dh, wd[0], (1, 1)).astype(BF16))
-        gg0 = dot(a0, dgate0, (0, 0)).astype(BF16)
-        gu0 = dot(a0, dup0, (0, 0)).astype(BF16)
-        gg0, gu0, gd0 = scatter((gg0, gu0, gd0), 0)
-        grads = [[g.astype(F32) for g in pair] for pair in ((gg0, gg1), (gu0, gu1), (gd0, gd1))]
-        total = total_of(sum(jnp.sum(g * g) for pair in grads for g in pair), 1)
+        spread = lambda g: lax.psum_scatter(g, "dp", scatter_dimension=0, tiled=True)
+        a0, gate0, up0, hid0 = up_layer(x, wg, wu, 0)
+        h1, a1 = down_layer(hid0, wd, x, 0)
+        hid1, dgate1, dup1 = turn_layer(a1, dy, wg, wu, wd, 1)
+        gd1 = spread(weight_grad(hid1, dy))
+        gg1 = spread(weight_grad(a1, dgate1))
+        gu1 = weight_grad(a1, dup1)
+        dh = back_layer(dgate1, dup1, wg, wu, h1, dy, 1)
+        gd0 = weight_grad(hid0, dh)
+        dgate0, dup0 = hidden_back(dh, wd, gate0, up0, 0)
+        gg0, gu0 = weight_grad(a0, dgate0), weight_grad(a0, dup0)
+        f, d = wg.shape[2], wd.shape[2]
+        thirds = [(3, k * (f // 3), f // 3, k) for k in range(3)]
+        gg0, gu0, gd0, gu1 = scatter((gg0, gu0, gd0, gu1), (*thirds, (2, 0, d, 2), (0, 0, f, 0), (1, 0, f, 1)), 0)
+        grads = ((gg0, gg1), (gu0, gu1), (gd0, gd1))
+        total = total_of([g for pair in grads for g in pair], 1)
         count = wg.size + wu.size + wd.size
         factor = jnp.minimum(1.0, 0.5 * lax.rsqrt(total / count + 1e-30))
         me = lax.axis_index("dp")
@@ -291,7 +442,7 @@
         for w, m, v, pair in zip((wg, wu, wd), moments[:3], moments[3:], grads):
             rows = w.shape[1] // n
             mine = lax.dynamic_slice_in_dim(w, me * rows, rows, 1)
-            g = jnp.stack(pair) * factor
+            g = jnp.stack(pair).astype(F32) * factor
             for to, value in zip((new_w, new_m, new_v), adamw(mine.astype(F32), m, v, g)):
                 to.append(value)
         new_w = gather(new_w, 2)

time: 768 us -> 697 us (0.908)
  matrix products: 391 us -> 0 us
  Pallas kernels: 254 us -> 628 us
  other arithmetic: 43.1 us -> 10.9 us
  local copies, waits for them, and re-layouts: 49.9 us -> 34.8 us
    dot_general x15 -> x0, matrix products: 391 us -> none  [dot(): lax.dot_general(a, b, ((contract[:1], contract[1:]), ((), ())), preferred...]
    pallas_call x2 -> x13, Pallas kernels: 97.3 us -> 471 us  [the longest x11 350 us: run(): pl.pallas_call(kernel, grid=grid, in_specs=[pl.BlockSpec(block, index) fo...]
    reduce_sum x7 -> x0, other arithmetic: 15 us -> none  [the longest x6 11.4 us: step(): total = total_of(sum((jnp.sum(g * g) for pair in grads for g in pair)), 1)]
    unnamed x37 -> x35, local copies, waits for them, and re-layouts: 48 us -> 33.6 us
    add x1 -> x0, other arithmetic: 12.3 us -> none  [step(): dh = dy + dwide.astype(BF16)]
  transfers between devices with their start and end apart: 3 -> 2, of which waited for: 0 -> 0; matrix products, arithmetic and copies ran while one was open for 31% -> 0% of each run, Pallas kernels for 12% -> 45%
where the time goes in v3:
time: 697 us; the launch traced here: 689 us
  Pallas kernels  628 us (90%)
  local copies, waits for them, and re-layouts  34.8 us (5%)
  between operations  15.4 us (2%)
  other arithmetic  10.9 us (2%)
    pallas_call x11, Pallas kernels, run(): pl.pallas_call(kernel, grid=grid, in_specs=[pl.BlockSpec(block, index) fo...  350 us
    pallas_call x1, Pallas kernels, gather(): pl.pallas_call(functools.partial(gather_kernel, count, layers), out_shape...  157 us
    pallas_call x1, Pallas kernels, scatter(): pl.pallas_call(functools.partial(scatter_kernel, count, jobs), out_shape=...  110 us
    unnamed x35, local copies, waits for them, and re-layouts  33.6 us
  transfers between devices with their start and end apart: 2, of which 0 were waited for; matrix products, arithmetic and copies ran while one was open for 0% of the time, Pallas kernels for 45%

profile of v3, /device:TPU:0, one launch (start us, length us, event | category | flops | bytes accessed | tf_op | source)
XLA Modules:
  0.0 689.3 jit_solution(2935324968604829514)
XLA Ops:
  7.2 48.8 %up.1 = (bf16[2048,1280]{1,0:T(8,128)(2,1)}, f32[2048,3072]{1,0:T(8,128)}, f32[2048,3072]{1,0:T(8,128)}, bf16[2048,3072]{1,0:T(8,128)(2,1)}) custom-call(bf16[2048,1280]{1,0:T(8,128)(2,1)} %bitcast.21, bf16[2,1280,3072]{2,1,0:T(8,128)(2,1)} %wg_ref.5, bf16[2,1280,3072]{2,1,0:T(8,128)(2,1)} %wu_ref.5), custom_call_target="tpu_custom_call" | custom-call | flops 32212254720 | bytes 36700160 | tf_op jit(solution)/shard_map/up/pallas_call | solution.py:272
  56.1 24.4 %down.1 = (bf16[2048,1280]{1,0:T(8,128)(2,1)}, bf16[2048,1280]{1,0:T(8,128)(2,1)}) custom-call(bf16[2048,3072]{1,0:T(8,128)(2,1)} %get-tuple-element.28.hid_ref.a_ref, bf16[2,3072,1280]{2,1,0:T(8,128)(2,1)} %wd_ref.3, bf16[2048,1280]{1,0:T(8,128)(2,1)} %bitcast.22), custom_call_target="tpu_custom_call" | custom-call | flops 16106127360 | bytes 33554432 | tf_op jit(solution)/shard_map/down/pallas_call | solution.py:272
  80.5 58.5 %turn.1 = (bf16[2048,3072]{1,0:T(8,128)(2,1)}, bf16[2048,3072]{1,0:T(8,128)(2,1)}, bf16[2048,3072]{1,0:T(8,128)(2,1)}) custom-call(bf16[2048,1280]{1,0:T(8,128)(2,1)} %get-tuple-element.29.a_ref, bf16[2048,1280]{1,0:T(8,128)(2,1)} %bitcast.23, bf16[2,1280,3072]{2,1,0:T(8,128)(2,1)} %wg_ref.5, bf16[2,1280,3072]{2,1,0:T(8,128)(2,1)} %wu_ref.5, ...), custom_call_target="tpu_custom_call" | custom-call | flops 48318382080 | bytes 57671680 | tf_op jit(solution)/shard_map/turn/pallas_call | solution.py:272
  139.0 22.1 %weight.10 = bf16[1280,3072]{1,0:T(8,128)(2,1)} custom-call(bf16[2048,1280]{1,0:T(8,128)(2,1)} %get-tuple-element.29.a_ref, bf16[2048,3072]{1,0:T(8,128)(2,1)} %get-tuple-element.30.dgate_ref.b_ref), custom_call_target="tpu_custom_call" | custom-call | flops 16106127360 | bytes 17825792 | tf_op jit(solution)/shard_map/weight/pallas_call | solution.py:272
  161.4 21.9 %weight.11 = bf16[3072,1280]{1,0:T(8,128)(2,1)} custom-call(bf16[2048,3072]{1,0:T(8,128)(2,1)} %get-tuple-element.41.a_ref, bf16[2048,1280]{1,0:T(8,128)(2,1)} %bitcast.24), custom_call_target="tpu_custom_call" | custom-call | flops 16106127360 | bytes 17825792 | tf_op jit(solution)/shard_map/weight/pallas_call | solution.py:272
  183.3 22.2 %weight.9 = bf16[1280,3072]{1,0:T(8,128)(2,1)} custom-call(bf16[2048,1280]{1,0:T(8,128)(2,1)} %get-tuple-element.29.a_ref, bf16[2048,3072]{1,0:T(8,128)(2,1)} %get-tuple-element.31.dup_ref.b_ref), custom_call_target="tpu_custom_call" | custom-call | flops 16106127360 | bytes 17825792 | tf_op jit(solution)/shard_map/weight/pallas_call | solution.py:272
  205.4 45.8 %back.1.dh_ref.b_ref = bf16[2048,1280]{1,0:T(8,128)(2,1)} custom-call(bf16[2048,3072]{1,0:T(8,128)(2,1)} %get-tuple-element.30.dgate_ref.b_ref, bf16[2048,3072]{1,0:T(8,128)(2,1)} %get-tuple-element.31.dup_ref.b_ref, bf16[2,1280,3072]{2,1,0:T(8,128)(2,1)} %wg_ref.5, bf16[2,1280,3072]{2,1,0:T(8,128)(2,1)} %wu_ref.5, ...), custom_call_target="tpu_custom_call" | custom-call | flops 32212254720 | bytes 67108864 | tf_op jit(solution)/shard_map/back/pallas_call | solution.py:272
  251.3 22.1 %weight.8 = bf16[3072,1280]{1,0:T(8,128)(2,1)} custom-call(bf16[2048,3072]{1,0:T(8,128)(2,1)} %get-tuple-element.28.hid_ref.a_ref, bf16[2048,1280]{1,0:T(8,128)(2,1)} %back.1.dh_ref.b_ref), custom_call_target="tpu_custom_call" | custom-call | flops 16106127360 | bytes 17825792 | tf_op jit(solution)/shard_map/weight/pallas_call | solution.py:272
  273.3 40.5 %hidden.1 = (bf16[2048,3072]{1,0:T(8,128)(2,1)}, bf16[2048,3072]{1,0:T(8,128)(2,1)}) custom-call(bf16[2048,1280]{1,0:T(8,128)(2,1)} %back.1.dh_ref.b_ref, bf16[2,3072,1280]{2,1,0:T(8,128)(2,1)} %wd_ref.3, f32[2048,3072]{1,0:T(8,128)} %get-tuple-element.33.gate_ref, f32[2048,3072]{1,0:T(8,128)} %get-tuple-element.34.up_ref), custom_call_target="tpu_custom_call" | custom-call | flops 16106127360 | bytes 71303168 | tf_op jit(solution)/shard_map/hidden/pallas_call | solution.py:272
  313.8 22.1 %weight.6 = bf16[1280,3072]{1,0:T(8,128)(2,1)} custom-call(bf16[2048,1280]{1,0:T(8,128)(2,1)} %get-tuple-element.27.a_ref, bf16[2048,3072]{1,0:T(8,128)(2,1)} %get-tuple-element.35.b_ref), custom_call_target="tpu_custom_call" | custom-call | flops 16106127360 | bytes 17825792 | tf_op jit(solution)/shard_map/weight/pallas_call | solution.py:272
  335.9 22.0 %weight.7 = bf16[1280,3072]{1,0:T(8,128)(2,1)} custom-call(bf16[2048,1280]{1,0:T(8,128)(2,1)} %get-tuple-element.27.a_ref, bf16[2048,3072]{1,0:T(8,128)(2,1)} %get-tuple-element.36.b_ref), custom_call_target="tpu_custom_call" | custom-call | flops 16106127360 | bytes 17825792 | tf_op jit(solution)/shard_map/weight/pallas_call | solution.py:272
  357.9 110.3 %scatter_0.1 = (bf16[80,3072]{1,0:T(8,128)(2,1)}, bf16[80,3072]{1,0:T(8,128)(2,1)}, bf16[192,1280]{1,0:T(8,128)(2,1)}, bf16[80,3072]{1,0:T(8,128)(2,1)}) custom-call(bf16[8,2,80,3072]{3,2,1,0:T(8,128)(2,1)} %bitcast.28, bf16[8,2,80,3072]{3,2,1,0:T(8,128)(2,1)} %bitcast.29, bf16[8,2,192,1280]{3,2,1,0:T(8,128)(2,1)} %bitcast.27, bf16[8,2,80,3072]{3,2,1,0:T(8,128)(2,1)} %bitcast.26), custom_call_target="tpu_custom_call" | custom-call | flops 10000000000 | bytes 29491200 | tf_op jit(solution)/shard_map/scatter_0/pallas_call | solution.py:112
  468.3 9.9 %total.1 = f32[8,128]{1,0:T(8,128)} custom-call(bf16[80,3072]{1,0:T(8,128)(2,1)} %get-tuple-element.37.refs_0_, bf16[80,3072]{1,0:T(8,128)(2,1)} %reduce-scatter.3.cloned.1.call-done.refs_1_, bf16[80,3072]{1,0:T(8,128)(2,1)} %get-tuple-element.38.refs_2_, bf16[80,3072]{1,0:T(8,128)(2,1)} %get-tuple-element.39.refs_3_, ...), custom_call_target="tpu_custom_call" | custom-call | tf_op jit(solution)/shard_map/total/pallas_call | solution.py:165
  478.2 1.2 slice.3
  480.2 4.9 fusion.8
  485.2 0.9 copy-done.10
  486.1 0.6 copy-done.11
  486.7 6.0 fusion.2
  492.7 157.2 %gather.1 = (bf16[2,1280,3072]{2,1,0:T(8,128)(2,1)}, bf16[2,1280,3072]{2,1,0:T(8,128)(2,1)}, bf16[2,3072,1280]{2,1,0:T(8,128)(2,1)}) custom-call(bf16[2,80,3072]{2,1,0:T(8,128)(2,1)} %get-tuple-element.51.refs_0_, bf16[2,80,3072]{2,1,0:T(8,128)(2,1)} %get-tuple-element.54.refs_1_, bf16[2,192,1280]{2,1,0:T(8,128)(2,1)} %get-tuple-element.45.refs_2_), custom_call_target="tpu_custom_call" | custom-call | flops 10000000000 | bytes 44236800 | tf_op jit(solution)/shard_map/gather/pallas_call | solution.py:235
  649.9 15.9 %copy.23 = bf16[2,1280,3072]{2,1,0:T(8,128)(2,1)} copy(bf16[2,1280,3072]{2,1,0:T(8,128)(2,1)} %get-tuple-element.66) | data formatting | bytes 31457280
  665.8 8.0 %copy.24 = bf16[2,1280,3072]{2,1,0:T(8,128)(2,1)} copy(bf16[2,1280,3072]{2,1,0:T(8,128)(2,1)S(1)} %copy-done) | data formatting | bytes 31457280
  673.8 1.5 slice-done.2
  675.3 0.9 slice-done.3
  676.2 5.8 copy.25
  (35 shorter events, 0.4 us)
Async XLA Ops:
  7.2 461.1 %reduce-scatter.3.cloned.1.call-start = ((), (), s32[]{:S(2)}) async-start(), calls=%async_computation.2 | async-start | bytes 8355840 | tf_op jit(solution)/shard_map/reduce_scatter | solution.py:422
  161.1 307.2 %reduce-scatter.5.cloned.1.call-start = ((), (), s32[]{:S(2)}) async-start(), calls=%async_computation.3 | async-start | bytes 8355840 | tf_op jit(solution)/shard_map/reduce_scatter | solution.py:422
  468.2 11.9 %copy-start.1 = (f32[2,192,1280]{2,1,0:T(8,128)S(1)}, f32[2,192,1280]{2,1,0:T(8,128)}, u32[]{:S(2)}) copy-start(f32[2,192,1280]{2,1,0:T(8,128)} %param.21) | copy-start | bytes 5898244
  468.2 11.9 %copy-start.7 = (bf16[192,1280]{1,0:T(8,128)(2,1)S(1)}, bf16[192,1280]{1,0:T(8,128)(2,1)}, u32[]{:S(2)}) copy-start(bf16[192,1280]{1,0:T(8,128)(2,1)} %get-tuple-element.40.refs_4_) | copy-start | bytes 1474564
  468.3 11.8 %copy-start.3 = (bf16[192,1280]{1,0:T(8,128)(2,1)S(1)}, bf16[192,1280]{1,0:T(8,128)(2,1)}, u32[]{:S(2)}) copy-start(bf16[192,1280]{1,0:T(8,128)(2,1)} %reduce-scatter.5.cloned.1.call-done.refs_5_) | copy-start | bytes 1474564
  480.1 5.0 copy-start.2
  480.1 5.0 copy-start.4
  480.1 5.0 copy-start.5
  480.2 5.0 copy-start.6
  480.2 5.0 copy-start.8
  480.2 5.0 copy-start.9
  480.2 5.9 copy-start.10
  480.2 6.5 copy-start.11
  649.9 15.9 %copy-start = (bf16[2,1280,3072]{2,1,0:T(8,128)(2,1)S(1)}, bf16[2,1280,3072]{2,1,0:T(8,128)(2,1)}, u32[]{:S(2)}) copy-start(bf16[2,1280,3072]{2,1,0:T(8,128)(2,1)} %get-tuple-element.67) | copy-start | bytes 47185924
  649.9 23.9 %slice-start = ((s8[15728640]{0:T(1024)(128)(4,1)}), s8[4194304]{0:T(1024)(128)(4,1)S(1)}, s32[]{:S(2)}) async-start(s8[15728640]{0:T(1024)(128)(4,1)} %bitcast.13), calls=%async_computation.4 | async-start | bytes 8388608
  649.9 23.9 %slice-start.1 = ((s8[15728640]{0:T(1024)(128)(4,1)}), s8[4194304]{0:T(1024)(128)(4,1)S(1)}, s32[]{:S(2)}) async-start(s8[15728640]{0:T(1024)(128)(4,1)} %bitcast.13), calls=%async_computation.5 | async-start | bytes 8388608
  665.8 9.5 %slice-start.2 = ((s8[15728640]{0:T(1024)(128)(4,1)}), s8[4194304]{0:T(1024)(128)(4,1)S(1)}, s32[]{:S(2)}) async-start(s8[15728640]{0:T(1024)(128)(4,1)} %bitcast.13), calls=%async_computation.6 | async-start | bytes 8388608
  665.8 10.4 %slice-start.3 = ((s8[15728640]{0:T(1024)(128)(4,1)}), s8[3145728]{0:T(1024)(128)(4,1)S(1)}, s32[]{:S(2)}) async-start(s8[15728640]{0:T(1024)(128)(4,1)} %bitcast.13), calls=%async_computation.7 | async-start | bytes 6291456
Sparse Core Ops, SparseCore 0:
  161.3 75.8 reduce-scatter.2
  241.5 72.9 reduce-scatter.4

commit v4 on v3

--- a/solution.py
+++ b/solution.py
@@ -54,71 +54,138 @@
     lax.fori_loop(0, rows // 16, body, 0)
 
 
-def scatter_kernel(count, jobs, *refs):
-    grads, outs, rest = refs[:count], refs[count : 2 * count], refs[2 * count :]
+STAGES = ((1, 3, 5, 7), (2, 6), (4,))
+
+
+def finish_kernel(cuts, d_ready, hid, dh, a, dgu, *refs):
+    outs, full, rest = refs[:4], (d_ready, *refs[4:7]), refs[7:]
+    jobs = [(q, start, width, turned(k)) for q in range(4) for k, (start, width) in enumerate(cuts[q])]
     n = len(jobs)
     own, paired, first, second, third = (rest[k * n : (k + 1) * n] for k in range(5))
-    local_sem, send_pair, recv_pair, send, recv = rest[5 * n :]
+    load_sem, send_pair, recv_pair, send, recv, weight_sem = rest[5 * n :]
     me = lax.axis_index("dp")
     core = lax.rem(me, 2)
     partner = flip(me, 1)
     near = [flip(me, bit) for bit in BITS]
     meet([*near, partner])
 
-    axes = [turned(turn) for _, _, _, turn in jobs]
-    loads, pairs, hops = {}, {}, {}
-    for mask in (1, 3, 5, 7, 2, 6, 4, 0):
-        for j, (i, start, width, _) in enumerate(jobs):
-            chip, columns = lax.div(flips(me, axes[j], mask), 2), pl.ds(start, width)
-            pairs[j, mask] = remote(
-                grads[i].at[chip, 1 - core, :, columns], paired[j].at[mask], send_pair.at[j, mask], recv_pair.at[j, mask], partner
-            )
-            pairs[j, mask].start()
-            loads[j, mask] = pltpu.make_async_copy(grads[i].at[chip, core, :, columns], own[j].at[mask], local_sem.at[j, mask])
-            loads[j, mask].start()
-
-    def hop(j, mask, stage):
+    def load(j):
+        q, start, width, _ = jobs[j]
+        return pltpu.make_async_copy(full[q].at[:, core, :, pl.ds(start, width)], own[j], load_sem.at[j])
+
+    def pair(j):
+        q, start, width, _ = jobs[j]
+        return remote(full[q].at[:, 1 - core, :, pl.ds(start, width)], paired[j], send_pair.at[j], recv_pair.at[j], partner)
+
+    def at(j, mask):
+        return lax.div(flips(me, jobs[j][3], mask), 2)
+
+    def stage_of(mask):
+        return 0 if mask & 1 else 1 if mask & 2 else 2
+
+    def hop(j, mask):
+        stage = stage_of(mask)
         dst = (first, second, third)[stage][j].at[mask >> (stage + 1)]
-        hops[j, mask] = remote(own[j].at[mask], dst, send.at[j, mask], recv.at[j, mask], near[axes[j][stage]])
-        hops[j, mask].start()
+        return remote(own[j].at[at(j, mask)], dst, send.at[j, mask], recv.at[j, mask], near[jobs[j][3][stage]])
 
     def add(j, mask, stage):
-        loads[j, mask].wait()
-        pairs[j, mask].wait_recv()
-        terms = [own[j].at[mask], paired[j].at[mask]]
+        terms = [own[j].at[at(j, mask)], paired[j].at[at(j, mask)]]
         for s in range(stage):
-            hops[j, mask + (1 << s)].wait_recv()
+            hop(j, mask + (1 << s)).wait_recv()
             terms.append((first, second, third)[s][j].at[mask >> (s + 1)])
-        i, start, width, _ = jobs[j]
-        sum_into(outs[i].at[:, pl.ds(start, width)] if mask == 0 else own[j].at[mask], terms, own[j].shape[1])
-
-    for stage, masks in enumerate(((1, 3, 5, 7), (2, 6), (4,))):
-        for mask in masks:
-            for j in range(n):
+        q, start, width, _ = jobs[j]
+        sum_into(own[j].at[at(j, mask)] if mask else outs[q].at[:, pl.ds(start, width)], terms, own[j].shape[1])
+
+    def begin(q):
+        for j in range(3 * q, 3 * q + 3):
+            pair(j).start()
+            load(j).start()
+
+    def go(q, stage):
+        for j in range(3 * q, 3 * q + 3):
+            if stage == 0:
+                load(j).wait()
+                pair(j).wait_recv()
+            for mask in STAGES[stage] if stage < 3 else (0,):
                 add(j, mask, stage)
-                hop(j, mask, stage)
+                if mask:
+                    hop(j, mask).start()
+
+    def matmuls(events, grid, ins, out, rhs=None):
+        def body(*tiles):
+            step = pl.program_id(0) * grid[1] + pl.program_id(1)
+            for when, what in events.items():
+
+                @pl.when(step == when)
+                def _(what=what):
+                    go(*what)
+
+            lhs, tile = tiles[0], tiles[-1]
+            right = tiles[1] if rhs is None else rhs
+            tile[...] = dot(lhs[...], right[...], (0, 0)).astype(BF16).reshape(tile.shape)
+
+        specs = [pl.BlockSpec(block, index) for _, block, index in ins]
+        pltpu.emit_pipeline(body, grid=grid, in_specs=specs, out_specs=[pl.BlockSpec(out[1], out[2])])(*[i[0] for i in ins], out[0])
+
+    begin(0)
+
+    def down(rhs):
+        copy = pltpu.make_async_copy(dh, rhs, weight_sem)
+        copy.start()
+        copy.wait()
+        t, p = hid.shape
+        rows, columns = full[1].shape[2:]
+        tp = 2 * 2 * rows
+        matmuls({3: (0, 0)}, (p // tp, 1), [(hid, (t, tp), lambda i, j: (0, i))], (full[1], (2, 2, rows, columns), lambda i, j: (i, 0, 0, 0)), rhs)
+
+    pl.run_scoped(down, pltpu.VMEM(dh.shape, BF16))
+    begin(1)
+    t, p = a.shape
+    rows, columns = full[2].shape[2:]
+    tp, tq = 4 * 2 * rows, 512
+    grid = (p // tp, columns // tq)
+    for q, events in ((2, {3: (0, 1), 6: (1, 0), 11: (0, 2)}), (3, {2: (0, 3), 4: (1, 1), 6: (2, 0), 11: (1, 2)})):
+        matmuls(
+            events,
+            grid,
+            [(a, (t, tp), lambda i, j: (0, i)), (dgu.at[q - 2], (t, tq), lambda i, j: (0, j))],
+            (full[q], (4, 2, rows, tq), lambda i, j: (i, 0, 0, j)),
+        )
+        begin(q)
+    for what in ((1, 3), (2, 1), (3, 0), (2, 2), (3, 1), (2, 3), (3, 2), (3, 3)):
+        go(*what)
     for j in range(n):
-        add(j, 0, 3)
-    for copy in (*pairs.values(), *hops.values()):
-        copy.wait_send()
-
-
-def scatter(grads, jobs, collective_id):
-    count = len(grads)
-    shapes = [(g.shape[0] // 16, g.shape[1]) for g in grads]
-    buffers = lambda n: [pltpu.VMEM((n, shapes[i][0], width), BF16) for i, _, width, _ in jobs]
-    sems = pltpu.SemaphoreType.DMA((len(jobs), 8))
-    sent = sum(r * c for r, c in shapes) * 2 * 15
+        pair(j).wait_send()
+        for mask in range(1, 8):
+            hop(j, mask).wait_send()
+
+
+def thirds(columns):
+    cuts, left = [], columns // 128
+    for k in (3, 2, 1):
+        cuts.append((columns - left * 128, left // k * 128))
+        left -= left // k
+    return tuple(cuts)
+
+
+def finish(ready, hid, dh, a, dgu, collective_id):
+    shapes = [(ready.shape[0] // 16, ready.shape[1]), (hid.shape[1] // 16, dh.shape[1]), *[(a.shape[1] // 16, dgu.shape[2])] * 2]
+    cuts = [thirds(columns) for _, columns in shapes]
+    buffers = lambda n: [pltpu.VMEM((n, rows, width), BF16) for (rows, _), cut in zip(shapes, cuts) for _, width in cut]
+    sems, one = pltpu.SemaphoreType.DMA((12, 8)), pltpu.SemaphoreType.DMA((12,))
+    blocked = [(8, 2, *shape) for shape in shapes]
     return pl.pallas_call(
-        functools.partial(scatter_kernel, count, jobs),
-        out_shape=[jax.ShapeDtypeStruct(shape, BF16) for shape in shapes],
-        in_specs=[IN_HBM] * count,
-        out_specs=[IN_VMEM] * count,
-        scratch_shapes=[*buffers(8), *buffers(8), *buffers(4), *buffers(2), *buffers(1), *[sems] * 5],
-        compiler_params=pltpu.CompilerParams(collective_id=collective_id, has_side_effects=True, vmem_limit_bytes=VMEM_BYTES),
-        cost_estimate=pl.CostEstimate(flops=10**10, bytes_accessed=sent, transcendentals=0),
-        name=f"scatter_{collective_id}",
-    )(*[g.reshape(8, 2, *shape) for g, shape in zip(grads, shapes)])
+        functools.partial(finish_kernel, cuts),
+        out_shape=[jax.ShapeDtypeStruct(shape, BF16) for shape in (*shapes, *blocked[1:])],
+        in_specs=[IN_HBM] * 5,
+        out_specs=[IN_VMEM] * 4 + [IN_HBM] * 3,
+        scratch_shapes=[
+            *buffers(8), *buffers(8), *buffers(4), *buffers(2), *buffers(1), one, one, one, sems, sems, pltpu.SemaphoreType.DMA
+        ],
+        compiler_params=pltpu.CompilerParams(collective_id=collective_id, has_side_effects=True, vmem_limit_bytes=67043328),
+        cost_estimate=pl.CostEstimate(flops=5 * 10**10, bytes_accessed=10**8, transcendentals=0),
+        name="finish",
+    )(ready.reshape(blocked[0]), hid, dh, a, dgu)[:4]
 
 
 def total_kernel(count, *refs):
@@ -374,22 +441,22 @@
     )[0]
 
 
-def hidden_kernel(dh_ref, wd_ref, gate_ref, up_ref, dgate_ref, dup_ref):
-    for at in pieces(gate_ref.shape[1], 256):
+def hidden_kernel(dh_ref, wd_ref, gate_ref, up_ref, both_ref):
+    for at in pieces(gate_ref.shape[1], 512):
         d = dot(dh_ref[...], wd_ref[0, at, :], (1, 1)).astype(BF16).astype(F32)
-        dgate_ref[:, at], dup_ref[:, at] = gated_back(gate_ref[:, at], up_ref[:, at], d)
+        both_ref[0, :, at], both_ref[1, :, at] = gated_back(gate_ref[:, at], up_ref[:, at], d)
 
 
 def hidden_back(dh, wd, gate, up, l):
     (t, d), f = dh.shape, gate.shape[1]
-    tm, tn = 1024, 512
-    row, tile = (lambda i, j: (i, 0)), (lambda i, j: (i, j))
+    tm = 256
+    row = lambda i: (i, 0)
     return run(
-        hidden_kernel, "hidden", (t // tm, f // tn),
-        [(dh, (tm, d), row), (wd, (1, tn, d), lambda i, j: (l, j, 0)), (gate, (tm, tn), tile), (up, (tm, tn), tile)],
-        [((t, f), BF16, (tm, tn), tile)] * 2,
+        hidden_kernel, "hidden", (t // tm,),
+        [(dh, (tm, d), row), (wd, (1, f, d), lambda i: (l, 0, 0)), (gate, (tm, f), row), (up, (tm, f), row)],
+        [((2, t, f), BF16, (2, tm, f), lambda i: (0, i, 0))],
         2 * t * d * f,
-    )
+    )[0]
 
 
 def weight_kernel(a_ref, b_ref, out_ref):
@@ -427,12 +494,8 @@
         gg1 = spread(weight_grad(a1, dgate1))
         gu1 = weight_grad(a1, dup1)
         dh = back_layer(dgate1, dup1, wg, wu, h1, dy, 1)
-        gd0 = weight_grad(hid0, dh)
-        dgate0, dup0 = hidden_back(dh, wd, gate0, up0, 0)
-        gg0, gu0 = weight_grad(a0, dgate0), weight_grad(a0, dup0)
-        f, d = wg.shape[2], wd.shape[2]
-        thirds = [(3, k * (f // 3), f // 3, k) for k in range(3)]
-        gg0, gu0, gd0, gu1 = scatter((gg0, gu0, gd0, gu1), (*thirds, (2, 0, d, 2), (0, 0, f, 0), (1, 0, f, 1)), 0)
+        dgu = hidden_back(dh, wd, gate0, up0, 0)
+        gu1, gd0, gg0, gu0 = finish(gu1, hid0, dh, a0, dgu, 0)
         grads = ((gg0, gg1), (gu0, gu1), (gd0, gd1))
         total = total_of([g for pair in grads for g in pair], 1)
         count = wg.size + wu.size + wd.size

time: 697 us -> 661 us (0.948)
  Pallas kernels: 628 us -> 591 us
    pallas_call x11 -> x8, Pallas kernels: 350 us -> 281 us  [run(): pl.pallas_call(kernel, grid=grid, in_specs=[pl.BlockSpec(block, index) fo...]
    pallas_call x1, Pallas kernels: 110 us -> 143 us  [finish(): pl.pallas_call(functools.partial(finish_kernel, cuts), out_shape=[jax.Sha...]
  transfers between devices with their start and end apart: 2 -> 2, of which waited for: 0 -> 0; matrix products, arithmetic and copies ran while one was open for 0% -> 0% of each run, Pallas kernels for 45% -> 41%
where the time goes in v4:
time: 661 us; the launch traced here: 653 us
  Pallas kernels  591 us (89%)
  local copies, waits for them, and re-layouts  34.8 us (5%)
  between operations  15.4 us (2%)
  other arithmetic  10.9 us (2%)
    pallas_call x8, Pallas kernels, run(): pl.pallas_call(kernel, grid=grid, in_specs=[pl.BlockSpec(block, index) fo...  281 us
    pallas_call x1, Pallas kernels, gather(): pl.pallas_call(functools.partial(gather_kernel, count, layers), out_shape...  157 us
    pallas_call x1, Pallas kernels, finish(): pl.pallas_call(functools.partial(finish_kernel, cuts), out_shape=[jax.Sha...  143 us
    unnamed x35, local copies, waits for them, and re-layouts  33.6 us
  transfers between devices with their start and end apart: 2, of which 0 were waited for; matrix products, arithmetic and copies ran while one was open for 0% of the time, Pallas kernels for 41%

profile of v4, /device:TPU:0, one launch (start us, length us, event | category | flops | bytes accessed | tf_op | source)
XLA Modules:
  0.0 652.8 jit_solution(7959105972982828838)
XLA Ops:
  7.2 0.0 reduce-scatter.3.cloned.1.call-start
  7.2 48.8 %up.1 = (bf16[2048,1280]{1,0:T(8,128)(2,1)}, f32[2048,3072]{1,0:T(8,128)}, f32[2048,3072]{1,0:T(8,128)}, bf16[2048,3072]{1,0:T(8,128)(2,1)}) custom-call(bf16[2048,1280]{1,0:T(8,128)(2,1)} %bitcast.18, bf16[2,1280,3072]{2,1,0:T(8,128)(2,1)} %wg_ref.5, bf16[2,1280,3072]{2,1,0:T(8,128)(2,1)} %wu_ref.5), custom_call_target="tpu_custom_call" | custom-call | flops 32212254720 | bytes 36700160 | tf_op jit(solution)/shard_map/up/pallas_call | solution.py:339
  56.1 24.4 %down.1 = (bf16[2048,1280]{1,0:T(8,128)(2,1)}, bf16[2048,1280]{1,0:T(8,128)(2,1)}) custom-call(bf16[2048,3072]{1,0:T(8,128)(2,1)} %get-tuple-element.25.hid_ref.hid, bf16[2,3072,1280]{2,1,0:T(8,128)(2,1)} %wd_ref.3, bf16[2048,1280]{1,0:T(8,128)(2,1)} %bitcast.19), custom_call_target="tpu_custom_call" | custom-call | flops 16106127360 | bytes 33554432 | tf_op jit(solution)/shard_map/down/pallas_call | solution.py:339
  80.4 58.5 %turn.1 = (bf16[2048,3072]{1,0:T(8,128)(2,1)}, bf16[2048,3072]{1,0:T(8,128)(2,1)}, bf16[2048,3072]{1,0:T(8,128)(2,1)}) custom-call(bf16[2048,1280]{1,0:T(8,128)(2,1)} %get-tuple-element.26.a_ref, bf16[2048,1280]{1,0:T(8,128)(2,1)} %bitcast.20, bf16[2,1280,3072]{2,1,0:T(8,128)(2,1)} %wg_ref.5, bf16[2,1280,3072]{2,1,0:T(8,128)(2,1)} %wu_ref.5, ...), custom_call_target="tpu_custom_call" | custom-call | flops 48318382080 | bytes 57671680 | tf_op jit(solution)/shard_map/turn/pallas_call | solution.py:339
  139.0 22.1 %weight.4 = bf16[1280,3072]{1,0:T(8,128)(2,1)} custom-call(bf16[2048,1280]{1,0:T(8,128)(2,1)} %get-tuple-element.26.a_ref, bf16[2048,3072]{1,0:T(8,128)(2,1)} %get-tuple-element.28.dgate_ref.b_ref), custom_call_target="tpu_custom_call" | custom-call | flops 16106127360 | bytes 17825792 | tf_op jit(solution)/shard_map/weight/pallas_call | solution.py:339
  161.1 0.2 reduce-scatter.5.cloned.1.call-start
  161.3 21.9 %weight.5 = bf16[3072,1280]{1,0:T(8,128)(2,1)} custom-call(bf16[2048,3072]{1,0:T(8,128)(2,1)} %get-tuple-element.37.a_ref, bf16[2048,1280]{1,0:T(8,128)(2,1)} %bitcast.21), custom_call_target="tpu_custom_call" | custom-call | flops 16106127360 | bytes 17825792 | tf_op jit(solution)/shard_map/weight/pallas_call | solution.py:339
  183.2 22.1 %weight.3 = bf16[1280,3072]{1,0:T(8,128)(2,1)} custom-call(bf16[2048,1280]{1,0:T(8,128)(2,1)} %get-tuple-element.26.a_ref, bf16[2048,3072]{1,0:T(8,128)(2,1)} %get-tuple-element.27.b_ref.dup_ref), custom_call_target="tpu_custom_call" | custom-call | flops 16106127360 | bytes 17825792 | tf_op jit(solution)/shard_map/weight/pallas_call | solution.py:339
  205.3 46.0 %back.1.dh_ref.dh = bf16[2048,1280]{1,0:T(8,128)(2,1)} custom-call(bf16[2048,3072]{1,0:T(8,128)(2,1)} %get-tuple-element.28.dgate_ref.b_ref, bf16[2048,3072]{1,0:T(8,128)(2,1)} %get-tuple-element.27.b_ref.dup_ref, bf16[2,1280,3072]{2,1,0:T(8,128)(2,1)} %wg_ref.5, bf16[2,1280,3072]{2,1,0:T(8,128)(2,1)} %wu_ref.5, bf16[2048,1280]{1,0:T(8,128)(2,1)} %get-tuple-element.29.h_ref, ...), custom_call_target="tpu_custom_call" | custom-call | flops 32212254720 | bytes 67108864 | tf_op jit(solution)/shard_map/back/pallas_call | solution.py:339
  251.4 37.5 %hidden.1.dgu = bf16[2,2048,3072]{2,1,0:T(8,128)(2,1)} custom-call(bf16[2048,1280]{1,0:T(8,128)(2,1)} %back.1.dh_ref.dh, bf16[2,3072,1280]{2,1,0:T(8,128)(2,1)} %wd_ref.3, f32[2048,3072]{1,0:T(8,128)} %get-tuple-element.31.gate_ref, f32[2048,3072]{1,0:T(8,128)} %get-tuple-element.32.up_ref), custom_call_target="tpu_custom_call" | custom-call | flops 16106127360 | bytes 71303168 | tf_op jit(solution)/shard_map/hidden/pallas_call | solution.py:339
  288.8 143.1 %finish.1 = (bf16[80,3072]{1,0:T(8,128)(2,1)}, bf16[192,1280]{1,0:T(8,128)(2,1)}, bf16[80,3072]{1,0:T(8,128)(2,1)}, bf16[80,3072]{1,0:T(8,128)(2,1)}, bf16[8,2,1...) custom-call(bf16[8,2,80,3072]{3,2,1,0:T(8,128)(2,1)} %bitcast.23, ...), custom_call_target="tpu_custom_call" | custom-call | flops 49999998976 | bytes 100000000 | tf_op jit(solution)/shard_map/finish/pallas_call | solution.py:177
  432.0 0.0 reduce-scatter.3.cloned.1.call-done.refs_1_
  432.1 9.9 %total.1 = f32[8,128]{1,0:T(8,128)} custom-call(bf16[80,3072]{1,0:T(8,128)(2,1)} %get-tuple-element.33.refs_0_, bf16[80,3072]{1,0:T(8,128)(2,1)} %reduce-scatter.3.cloned.1.call-done.refs_1_, bf16[80,3072]{1,0:T(8,128)(2,1)} %get-tuple-element.34.refs_2_, bf16[80,3072]{1,0:T(8,128)(2,1)} %get-tuple-element.35.refs_3_, ...), custom_call_target="tpu_custom_call" | custom-call | tf_op jit(solution)/shard_map/total/pallas_call | solution.py:232
  441.9 1.2 slice.3
  443.9 4.9 fusion.8
  448.9 0.9 copy-done.10
  449.8 0.6 copy-done.11
  450.4 6.0 fusion.2
  456.4 157.0 %gather.1 = (bf16[2,1280,3072]{2,1,0:T(8,128)(2,1)}, bf16[2,1280,3072]{2,1,0:T(8,128)(2,1)}, bf16[2,3072,1280]{2,1,0:T(8,128)(2,1)}) custom-call(bf16[2,80,3072]{2,1,0:T(8,128)(2,1)} %get-tuple-element.47.refs_0_, bf16[2,80,3072]{2,1,0:T(8,128)(2,1)} %get-tuple-element.50.refs_1_, bf16[2,192,1280]{2,1,0:T(8,128)(2,1)} %get-tuple-element.41.refs_2_), custom_call_target="tpu_custom_call" | custom-call | flops 10000000000 | bytes 44236800 | tf_op jit(solution)/shard_map/gather/pallas_call | solution.py:302
  613.5 15.9 %copy.23 = bf16[2,1280,3072]{2,1,0:T(8,128)(2,1)} copy(bf16[2,1280,3072]{2,1,0:T(8,128)(2,1)} %get-tuple-element.62) | data formatting | bytes 31457280
  629.4 8.0 %copy.24 = bf16[2,1280,3072]{2,1,0:T(8,128)(2,1)} copy(bf16[2,1280,3072]{2,1,0:T(8,128)(2,1)S(1)} %copy-done) | data formatting | bytes 31457280
  637.4 1.5 slice-done.2
  638.9 0.9 slice-done.3
  639.8 5.8 copy.25
  (32 shorter events, 0.1 us)
Async XLA Ops:
  7.2 424.8 %reduce-scatter.3.cloned.1.call-start = ((), (), s32[]{:S(2)}) async-start(), calls=%async_computation.2 | async-start | bytes 8355840 | tf_op jit(solution)/shard_map/reduce_scatter | solution.py:489
  161.1 270.9 %reduce-scatter.5.cloned.1.call-start = ((), (), s32[]{:S(2)}) async-start(), calls=%async_computation.3 | async-start | bytes 8355840 | tf_op jit(solution)/shard_map/reduce_scatter | solution.py:489
  432.0 11.8 %copy-start.1 = (f32[2,192,1280]{2,1,0:T(8,128)S(1)}, f32[2,192,1280]{2,1,0:T(8,128)}, u32[]{:S(2)}) copy-start(f32[2,192,1280]{2,1,0:T(8,128)} %param.21) | copy-start | bytes 5898244
  432.0 11.8 %copy-start.7 = (bf16[192,1280]{1,0:T(8,128)(2,1)S(1)}, bf16[192,1280]{1,0:T(8,128)(2,1)}, u32[]{:S(2)}) copy-start(bf16[192,1280]{1,0:T(8,128)(2,1)} %get-tuple-element.36.refs_4_) | copy-start | bytes 1474564
  432.0 11.8 %copy-start.3 = (bf16[192,1280]{1,0:T(8,128)(2,1)S(1)}, bf16[192,1280]{1,0:T(8,128)(2,1)}, u32[]{:S(2)}) copy-start(bf16[192,1280]{1,0:T(8,128)(2,1)} %reduce-scatter.5.cloned.1.call-done.refs_5_) | copy-start | bytes 1474564
  443.8 5.0 copy-start.2
  443.8 5.0 copy-start.4
  443.9 5.0 copy-start.5
  443.9 5.0 copy-start.6
  443.9 5.0 copy-start.8
  443.9 5.0 copy-start.9
  443.9 5.9 copy-start.10
  443.9 6.5 copy-start.11
  613.5 15.9 %copy-start = (bf16[2,1280,3072]{2,1,0:T(8,128)(2,1)S(1)}, bf16[2,1280,3072]{2,1,0:T(8,128)(2,1)}, u32[]{:S(2)}) copy-start(bf16[2,1280,3072]{2,1,0:T(8,128)(2,1)} %get-tuple-element.63) | copy-start | bytes 47185924
  613.5 23.9 %slice-start = ((s8[15728640]{0:T(1024)(128)(4,1)}), s8[4194304]{0:T(1024)(128)(4,1)S(1)}, s32[]{:S(2)}) async-start(s8[15728640]{0:T(1024)(128)(4,1)} %bitcast.10), calls=%async_computation.4 | async-start | bytes 8388608
  613.5 23.9 %slice-start.1 = ((s8[15728640]{0:T(1024)(128)(4,1)}), s8[4194304]{0:T(1024)(128)(4,1)S(1)}, s32[]{:S(2)}) async-start(s8[15728640]{0:T(1024)(128)(4,1)} %bitcast.10), calls=%async_computation.5 | async-start | bytes 8388608
  629.4 9.5 %slice-start.2 = ((s8[15728640]{0:T(1024)(128)(4,1)}), s8[4194304]{0:T(1024)(128)(4,1)S(1)}, s32[]{:S(2)}) async-start(s8[15728640]{0:T(1024)(128)(4,1)} %bitcast.10), calls=%async_computation.6 | async-start | bytes 8388608
  629.4 10.4 %slice-start.3 = ((s8[15728640]{0:T(1024)(128)(4,1)}), s8[3145728]{0:T(1024)(128)(4,1)S(1)}, s32[]{:S(2)}) async-start(s8[15728640]{0:T(1024)(128)(4,1)} %bitcast.10), calls=%async_computation.7 | async-start | bytes 6291456
Sparse Core Ops, SparseCore 0:
  161.2 75.8 reduce-scatter.2
  241.5 73.6 reduce-scatter.4

commit v5 on v4

--- a/solution.py
+++ b/solution.py
@@ -57,9 +57,9 @@
 STAGES = ((1, 3, 5, 7), (2, 6), (4,))
 
 
-def finish_kernel(cuts, d_ready, hid, dh, a, dgu, *refs):
-    outs, full, rest = refs[:4], (d_ready, *refs[4:7]), refs[7:]
-    jobs = [(q, start, width, turned(k)) for q in range(4) for k, (start, width) in enumerate(cuts[q])]
+def finish_kernel(cuts, hid, dh, a, dgu, *refs):
+    outs, full, rest = refs[:3], refs[3:6], refs[6:]
+    jobs = [(q, start, width, turned(k)) for q in range(3) for k, (start, width) in enumerate(cuts[q])]
     n = len(jobs)
     own, paired, first, second, third = (rest[k * n : (k + 1) * n] for k in range(5))
     load_sem, send_pair, recv_pair, send, recv, weight_sem = rest[5 * n :]
@@ -127,32 +127,30 @@
         specs = [pl.BlockSpec(block, index) for _, block, index in ins]
         pltpu.emit_pipeline(body, grid=grid, in_specs=specs, out_specs=[pl.BlockSpec(out[1], out[2])])(*[i[0] for i in ins], out[0])
 
-    begin(0)
-
     def down(rhs):
         copy = pltpu.make_async_copy(dh, rhs, weight_sem)
         copy.start()
         copy.wait()
         t, p = hid.shape
-        rows, columns = full[1].shape[2:]
+        rows, columns = full[0].shape[2:]
         tp = 2 * 2 * rows
-        matmuls({3: (0, 0)}, (p // tp, 1), [(hid, (t, tp), lambda i, j: (0, i))], (full[1], (2, 2, rows, columns), lambda i, j: (i, 0, 0, 0)), rhs)
+        matmuls({}, (p // tp, 1), [(hid, (t, tp), lambda i, j: (0, i))], (full[0], (2, 2, rows, columns), lambda i, j: (i, 0, 0, 0)), rhs)
 
     pl.run_scoped(down, pltpu.VMEM(dh.shape, BF16))
-    begin(1)
+    begin(0)
     t, p = a.shape
-    rows, columns = full[2].shape[2:]
-    tp, tq = 4 * 2 * rows, 512
+    rows, columns = full[1].shape[2:]
+    tp, tq = 4 * 2 * rows, 1024
     grid = (p // tp, columns // tq)
-    for q, events in ((2, {3: (0, 1), 6: (1, 0), 11: (0, 2)}), (3, {2: (0, 3), 4: (1, 1), 6: (2, 0), 11: (1, 2)})):
+    for q, events in ((1, {3: (0, 0)}), (2, {2: (0, 1), 3: (1, 0), 5: (0, 2)})):
         matmuls(
             events,
             grid,
-            [(a, (t, tp), lambda i, j: (0, i)), (dgu.at[q - 2], (t, tq), lambda i, j: (0, j))],
+            [(a, (t, tp), lambda i, j: (0, i)), (dgu.at[q - 1], (t, tq), lambda i, j: (0, j))],
             (full[q], (4, 2, rows, tq), lambda i, j: (i, 0, 0, j)),
         )
         begin(q)
-    for what in ((1, 3), (2, 1), (3, 0), (2, 2), (3, 1), (2, 3), (3, 2), (3, 3)):
+    for what in ((0, 3), (1, 1), (2, 0), (1, 2), (2, 1), (1, 3), (2, 2), (2, 3)):
         go(*what)
     for j in range(n):
         pair(j).wait_send()
@@ -168,24 +166,24 @@
     return tuple(cuts)
 
 
-def finish(ready, hid, dh, a, dgu, collective_id):
-    shapes = [(ready.shape[0] // 16, ready.shape[1]), (hid.shape[1] // 16, dh.shape[1]), *[(a.shape[1] // 16, dgu.shape[2])] * 2]
+def finish(hid, dh, a, dgu, collective_id):
+    shapes = [(hid.shape[1] // 16, dh.shape[1]), *[(a.shape[1] // 16, dgu.shape[2])] * 2]
     cuts = [thirds(columns) for _, columns in shapes]
     buffers = lambda n: [pltpu.VMEM((n, rows, width), BF16) for (rows, _), cut in zip(shapes, cuts) for _, width in cut]
-    sems, one = pltpu.SemaphoreType.DMA((12, 8)), pltpu.SemaphoreType.DMA((12,))
+    sems, one = pltpu.SemaphoreType.DMA((9, 8)), pltpu.SemaphoreType.DMA((9,))
     blocked = [(8, 2, *shape) for shape in shapes]
     return pl.pallas_call(
         functools.partial(finish_kernel, cuts),
-        out_shape=[jax.ShapeDtypeStruct(shape, BF16) for shape in (*shapes, *blocked[1:])],
-        in_specs=[IN_HBM] * 5,
-        out_specs=[IN_VMEM] * 4 + [IN_HBM] * 3,
+        out_shape=[jax.ShapeDtypeStruct(shape, BF16) for shape in (*shapes, *blocked)],
+        in_specs=[IN_HBM] * 4,
+        out_specs=[IN_VMEM] * 3 + [IN_HBM] * 3,
         scratch_shapes=[
             *buffers(8), *buffers(8), *buffers(4), *buffers(2), *buffers(1), one, one, one, sems, sems, pltpu.SemaphoreType.DMA
         ],
         compiler_params=pltpu.CompilerParams(collective_id=collective_id, has_side_effects=True, vmem_limit_bytes=67043328),
         cost_estimate=pl.CostEstimate(flops=5 * 10**10, bytes_accessed=10**8, transcendentals=0),
         name="finish",
-    )(ready.reshape(blocked[0]), hid, dh, a, dgu)[:4]
+    )(hid, dh, a, dgu)[:3]
 
 
 def total_kernel(count, *refs):
@@ -492,10 +490,10 @@
         hid1, dgate1, dup1 = turn_layer(a1, dy, wg, wu, wd, 1)
         gd1 = spread(weight_grad(hid1, dy))
         gg1 = spread(weight_grad(a1, dgate1))
-        gu1 = weight_grad(a1, dup1)
+        gu1 = spread(weight_grad(a1, dup1))
         dh = back_layer(dgate1, dup1, wg, wu, h1, dy, 1)
         dgu = hidden_back(dh, wd, gate0, up0, 0)
-        gu1, gd0, gg0, gu0 = finish(gu1, hid0, dh, a0, dgu, 0)
+        gd0, gg0, gu0 = finish(hid0, dh, a0, dgu, 0)
         grads = ((gg0, gg1), (gu0, gu1), (gd0, gd1))
         total = total_of([g for pair in grads for g in pair], 1)
         count = wg.size + wu.size + wd.size

time: 661 us -> 671 us (1.015)
  Pallas kernels: 591 us -> 602 us
    pallas_call x1, Pallas kernels: 143 us -> 153 us  [finish(): pl.pallas_call(functools.partial(finish_kernel, cuts), out_shape=[jax.Sha...]
  transfers between devices with their start and end apart: 2 -> 3, of which waited for: 0 -> 0; matrix products, arithmetic and copies ran while one was open for 0% -> 0% of each run, Pallas kernels for 41% -> 42%
where the time goes in v5:
time: 671 us; the launch traced here: 663 us
  Pallas kernels  602 us (90%)
  local copies, waits for them, and re-layouts  34.8 us (5%)
  between operations  15.1 us (2%)
  other arithmetic  10.9 us (2%)
    pallas_call x8, Pallas kernels, run(): pl.pallas_call(kernel, grid=grid, in_specs=[pl.BlockSpec(block, index) fo...  282 us
    pallas_call x1, Pallas kernels, gather(): pl.pallas_call(functools.partial(gather_kernel, count, layers), out_shape...  157 us
    pallas_call x1, Pallas kernels, finish(): pl.pallas_call(functools.partial(finish_kernel, cuts), out_shape=[jax.Sha...  153 us
    unnamed x35, local copies, waits for them, and re-layouts  33.6 us
  transfers between devices with their start and end apart: 3, of which 0 were waited for; matrix products, arithmetic and copies ran while one was open for 0% of the time, Pallas kernels for 42%

profile of v5, /device:TPU:0, one launch (start us, length us, event | category | flops | bytes accessed | tf_op | source)
XLA Modules:
  0.0 662.9 jit_solution(212915320455671694)
XLA Ops:
  7.2 0.0 reduce-scatter.4.cloned.1.call-start
  7.2 48.8 %up.1 = (bf16[2048,1280]{1,0:T(8,128)(2,1)}, f32[2048,3072]{1,0:T(8,128)}, f32[2048,3072]{1,0:T(8,128)}, bf16[2048,3072]{1,0:T(8,128)(2,1)}) custom-call(bf16[2048,1280]{1,0:T(8,128)(2,1)} %bitcast.17, bf16[2,1280,3072]{2,1,0:T(8,128)(2,1)} %wg_ref.5, bf16[2,1280,3072]{2,1,0:T(8,128)(2,1)} %wu_ref.5), custom_call_target="tpu_custom_call" | custom-call | flops 32212254720 | bytes 36700160 | tf_op jit(solution)/shard_map/up/pallas_call | solution.py:337
  56.1 24.4 %down.1 = (bf16[2048,1280]{1,0:T(8,128)(2,1)}, bf16[2048,1280]{1,0:T(8,128)(2,1)}) custom-call(bf16[2048,3072]{1,0:T(8,128)(2,1)} %get-tuple-element.24.hid_ref.hid, bf16[2,3072,1280]{2,1,0:T(8,128)(2,1)} %wd_ref.3, bf16[2048,1280]{1,0:T(8,128)(2,1)} %bitcast.18), custom_call_target="tpu_custom_call" | custom-call | flops 16106127360 | bytes 33554432 | tf_op jit(solution)/shard_map/down/pallas_call | solution.py:337
  80.4 58.5 %turn.1 = (bf16[2048,3072]{1,0:T(8,128)(2,1)}, bf16[2048,3072]{1,0:T(8,128)(2,1)}, bf16[2048,3072]{1,0:T(8,128)(2,1)}) custom-call(bf16[2048,1280]{1,0:T(8,128)(2,1)} %get-tuple-element.25.a_ref, bf16[2048,1280]{1,0:T(8,128)(2,1)} %bitcast.19, bf16[2,1280,3072]{2,1,0:T(8,128)(2,1)} %wg_ref.5, bf16[2,1280,3072]{2,1,0:T(8,128)(2,1)} %wu_ref.5, ...), custom_call_target="tpu_custom_call" | custom-call | flops 48318382080 | bytes 57671680 | tf_op jit(solution)/shard_map/turn/pallas_call | solution.py:337
  139.0 22.1 %weight.3 = bf16[1280,3072]{1,0:T(8,128)(2,1)} custom-call(bf16[2048,1280]{1,0:T(8,128)(2,1)} %get-tuple-element.25.a_ref, bf16[2048,3072]{1,0:T(8,128)(2,1)} %get-tuple-element.26.dgate_ref.b_ref), custom_call_target="tpu_custom_call" | custom-call | flops 16106127360 | bytes 17825792 | tf_op jit(solution)/shard_map/weight/pallas_call | solution.py:337
  161.1 0.2 reduce-scatter.6.cloned.1.call-start
  161.3 22.2 %weight.4 = bf16[1280,3072]{1,0:T(8,128)(2,1)} custom-call(bf16[2048,1280]{1,0:T(8,128)(2,1)} %get-tuple-element.25.a_ref, bf16[2048,3072]{1,0:T(8,128)(2,1)} %get-tuple-element.27.dup_ref.b_ref), custom_call_target="tpu_custom_call" | custom-call | flops 16106127360 | bytes 17825792 | tf_op jit(solution)/shard_map/weight/pallas_call | solution.py:337
  183.6 0.0 reduce-scatter.8.cloned.1.call-start
  183.6 21.9 %weight.5 = bf16[3072,1280]{1,0:T(8,128)(2,1)} custom-call(bf16[2048,3072]{1,0:T(8,128)(2,1)} %get-tuple-element.35.a_ref, bf16[2048,1280]{1,0:T(8,128)(2,1)} %bitcast.20), custom_call_target="tpu_custom_call" | custom-call | flops 16106127360 | bytes 17825792 | tf_op jit(solution)/shard_map/weight/pallas_call | solution.py:337
  205.5 46.3 %back.1.dh_ref.dh = bf16[2048,1280]{1,0:T(8,128)(2,1)} custom-call(bf16[2048,3072]{1,0:T(8,128)(2,1)} %get-tuple-element.26.dgate_ref.b_ref, bf16[2048,3072]{1,0:T(8,128)(2,1)} %get-tuple-element.27.dup_ref.b_ref, bf16[2,1280,3072]{2,1,0:T(8,128)(2,1)} %wg_ref.5, bf16[2,1280,3072]{2,1,0:T(8,128)(2,1)} %wu_ref.5, bf16[2048,1280]{1,0:T(8,128)(2,1)} %get-tuple-element.28.h_ref, ...), custom_call_target="tpu_custom_call" | custom-call | flops 32212254720 | bytes 67108864 | tf_op jit(solution)/shard_map/back/pallas_call | solution.py:337
  251.8 37.5 %hidden.1.dgu = bf16[2,2048,3072]{2,1,0:T(8,128)(2,1)} custom-call(bf16[2048,1280]{1,0:T(8,128)(2,1)} %back.1.dh_ref.dh, bf16[2,3072,1280]{2,1,0:T(8,128)(2,1)} %wd_ref.3, f32[2048,3072]{1,0:T(8,128)} %get-tuple-element.30.gate_ref, f32[2048,3072]{1,0:T(8,128)} %get-tuple-element.31.up_ref), custom_call_target="tpu_custom_call" | custom-call | flops 16106127360 | bytes 71303168 | tf_op jit(solution)/shard_map/hidden/pallas_call | solution.py:337
  289.3 152.9 %finish.1 = (bf16[192,1280]{1,0:T(8,128)(2,1)}, bf16[80,3072]{1,0:T(8,128)(2,1)}, bf16[80,3072]{1,0:T(8,128)(2,1)}, bf16[8,2,192,1280]{3,2,1,0:T(8,128)(2,1)}, b...) custom-call(bf16[2048,3072]{1,0:T(8,128)(2,1)} %get-tuple-element.24.hid_ref.hid, ...), custom_call_target="tpu_custom_call" | custom-call | flops 49999998976 | bytes 100000000 | tf_op jit(solution)/shard_map/finish/pallas_call | solution.py:175
  442.3 9.9 %total.1 = f32[8,128]{1,0:T(8,128)} custom-call(bf16[80,3072]{1,0:T(8,128)(2,1)} %get-tuple-element.32.refs_0_, bf16[80,3072]{1,0:T(8,128)(2,1)} %reduce-scatter.4.cloned.1.call-done.refs_1_, bf16[80,3072]{1,0:T(8,128)(2,1)} %get-tuple-element.33.refs_2_, bf16[80,3072]{1,0:T(8,128)(2,1)} %reduce-scatter.6.cloned.1.call-done.refs_3_, ...), custom_call_target="tpu_custom_call" | custom-call | tf_op jit(solution)/shard_map/total/pallas_call | solution.py:230
  452.2 1.2 slice.3
  454.2 4.9 fusion.8
  459.2 0.9 copy-done.10
  460.0 0.6 copy-done.11
  460.7 6.0 fusion.2
  466.7 157.2 %gather.1 = (bf16[2,1280,3072]{2,1,0:T(8,128)(2,1)}, bf16[2,1280,3072]{2,1,0:T(8,128)(2,1)}, bf16[2,3072,1280]{2,1,0:T(8,128)(2,1)}) custom-call(bf16[2,80,3072]{2,1,0:T(8,128)(2,1)} %get-tuple-element.45.refs_0_, bf16[2,80,3072]{2,1,0:T(8,128)(2,1)} %get-tuple-element.48.refs_1_, bf16[2,192,1280]{2,1,0:T(8,128)(2,1)} %get-tuple-element.39.refs_2_), custom_call_target="tpu_custom_call" | custom-call | flops 10000000000 | bytes 44236800 | tf_op jit(solution)/shard_map/gather/pallas_call | solution.py:300
  623.9 15.9 %copy.23 = bf16[2,1280,3072]{2,1,0:T(8,128)(2,1)} copy(bf16[2,1280,3072]{2,1,0:T(8,128)(2,1)} %get-tuple-element.60) | data formatting | bytes 31457280
  639.8 8.0 %copy.24 = bf16[2,1280,3072]{2,1,0:T(8,128)(2,1)} copy(bf16[2,1280,3072]{2,1,0:T(8,128)(2,1)S(1)} %copy-done) | data formatting | bytes 31457280
  647.8 1.5 slice-done.2
  649.3 0.9 slice-done.3
  650.2 5.8 copy.25
  (35 shorter events, 0.2 us)
Async XLA Ops:
  7.2 435.1 %reduce-scatter.4.cloned.1.call-start = ((), (), s32[]{:S(2)}) async-start(), calls=%async_computation.3 | async-start | bytes 8355840 | tf_op jit(solution)/shard_map/reduce_scatter | solution.py:487
  161.1 281.2 %reduce-scatter.6.cloned.1.call-start = ((), (), s32[]{:S(2)}) async-start(), calls=%async_computation.4 | async-start | bytes 8355840 | tf_op jit(solution)/shard_map/reduce_scatter | solution.py:487
  183.6 258.7 %reduce-scatter.8.cloned.1.call-start = ((), (), s32[]{:S(2)}) async-start(), calls=%async_computation.5 | async-start | bytes 8355840 | tf_op jit(solution)/shard_map/reduce_scatter | solution.py:487
  442.2 11.9 %copy-start.1 = (f32[2,192,1280]{2,1,0:T(8,128)S(1)}, f32[2,192,1280]{2,1,0:T(8,128)}, u32[]{:S(2)}) copy-start(f32[2,192,1280]{2,1,0:T(8,128)} %param.21) | copy-start | bytes 5898244
  442.2 11.9 %copy-start.7 = (bf16[192,1280]{1,0:T(8,128)(2,1)S(1)}, bf16[192,1280]{1,0:T(8,128)(2,1)}, u32[]{:S(2)}) copy-start(bf16[192,1280]{1,0:T(8,128)(2,1)} %get-tuple-element.34.refs_4_) | copy-start | bytes 1474564
  442.3 11.8 %copy-start.4 = (bf16[192,1280]{1,0:T(8,128)(2,1)S(1)}, bf16[192,1280]{1,0:T(8,128)(2,1)}, u32[]{:S(2)}) copy-start(bf16[192,1280]{1,0:T(8,128)(2,1)} %reduce-scatter.8.cloned.1.call-done.refs_5_) | copy-start | bytes 1474564
  454.1 5.0 copy-start.2
  454.1 5.0 copy-start.3
  454.1 5.0 copy-start.5
  454.1 5.0 copy-start.6
  454.1 5.0 copy-start.8
  454.2 5.0 copy-start.9
  454.2 5.9 copy-start.10
  454.2 6.5 copy-start.11
  623.9 15.9 %copy-start = (bf16[2,1280,3072]{2,1,0:T(8,128)(2,1)S(1)}, bf16[2,1280,3072]{2,1,0:T(8,128)(2,1)}, u32[]{:S(2)}) copy-start(bf16[2,1280,3072]{2,1,0:T(8,128)(2,1)} %get-tuple-element.61) | copy-start | bytes 47185924
  623.9 23.9 %slice-start = ((s8[15728640]{0:T(1024)(128)(4,1)}), s8[4194304]{0:T(1024)(128)(4,1)S(1)}, s32[]{:S(2)}) async-start(s8[15728640]{0:T(1024)(128)(4,1)} %bitcast.9), calls=%async_computation.6 | async-start | bytes 8388608
  623.9 23.9 %slice-start.1 = ((s8[15728640]{0:T(1024)(128)(4,1)}), s8[4194304]{0:T(1024)(128)(4,1)S(1)}, s32[]{:S(2)}) async-start(s8[15728640]{0:T(1024)(128)(4,1)} %bitcast.9), calls=%async_computation.7 | async-start | bytes 8388608
  639.8 9.5 %slice-start.2 = ((s8[15728640]{0:T(1024)(128)(4,1)}), s8[4194304]{0:T(1024)(128)(4,1)S(1)}, s32[]{:S(2)}) async-start(s8[15728640]{0:T(1024)(128)(4,1)} %bitcast.9), calls=%async_computation.8 | async-start | bytes 8388608
  639.8 10.4 %slice-start.3 = ((s8[15728640]{0:T(1024)(128)(4,1)}), s8[3145728]{0:T(1024)(128)(4,1)S(1)}, s32[]{:S(2)}) async-start(s8[15728640]{0:T(1024)(128)(4,1)} %bitcast.9), calls=%async_computation.9 | async-start | bytes 6291456
Sparse Core Ops, SparseCore 0:
  161.2 75.8 reduce-scatter.3
  241.5 72.9 reduce-scatter.5
  319.0 96.1 reduce-scatter.7
